TPU v7x, 32 devices: a whole 2x2x4 slice. The times are simulated.
32 devices in a mesh: dp: 2 (over x), tp: 4 (over z), cp: 4 (over y, core).
Axes of the slice: x: 2, y: 2, z: 4, core: 2. Of those that a mesh axis runs over, the one named last changes fastest.
Arguments:
- hidden: bfloat16 [4096, 8192], P(('dp', 'cp')), parts along dimension 0
- positions: int32 [4096], P(('dp', 'cp')), parts along dimension 0
- norm_gain: bfloat16 [8192], replicated
- w_query: bfloat16 [8192, 8192], P(None, 'tp')
- w_key: bfloat16 [8192, 1024], P(None, 'tp')
- w_value: bfloat16 [8192, 1024], P(None, 'tp')
- w_out: bfloat16 [8192, 8192], P('tp')
Outputs:
- output 1: bfloat16 [4096, 8192], P(('dp', 'cp')), parts along dimension 0
- output 2: bfloat16 [4096, 8, 128], P(('dp', 'cp'), 'tp'), parts along dimension 0
- output 3: bfloat16 [4096, 8, 128], P(('dp', 'cp'), 'tp'), parts along dimension 0
There are 2 independent parts. A program takes and returns all parts, laid end to end along the dimension named above; an argument that names none is the same for every part.
All inputs are finite; a program needn't handle non-finite values.
Results may differ from a plain program's by a relative error of at most 0.00860334.
Values are sent between devices in bfloat16 or wider.
A program may use at most 1 GiB of HBM per device.

v0:
```python
import math
import jax
import jax.numpy as jnp
from jax import lax
from jax.sharding import PartitionSpec as P

HEAD = 128
EPS = 1e-5
LOG_THETA = math.log(1000000.0)
SCORE_SCALE = 1.0 / math.sqrt(HEAD)


def rms_norm(hidden, norm_gain):
    hidden_f = hidden.astype(jnp.float32)
    inv_rms = lax.rsqrt(jnp.mean(hidden_f * hidden_f, axis=-1, keepdims=True) + EPS)
    return (hidden_f * inv_rms * norm_gain.astype(jnp.float32)).astype(jnp.bfloat16)


def rope_tables(positions):
    half_dim = HEAD // 2
    inv_freq = jnp.exp(jnp.arange(half_dim, dtype=jnp.float32) * (-2.0 * LOG_THETA / HEAD))
    angles = positions.astype(jnp.float32)[..., None] * inv_freq
    return jnp.cos(angles), jnp.sin(angles)


def apply_rope(head_vals, cos_t, sin_t):
    half_dim = HEAD // 2
    first_half = head_vals[..., :half_dim]
    second_half = head_vals[..., half_dim:]
    return jnp.concatenate([first_half * cos_t - second_half * sin_t, second_half * cos_t + first_half * sin_t], axis=-1)


def project_heads(hidden, positions, norm_gain, w_query, w_key, w_value):
    row_count = hidden.shape[0]
    kv_local = w_key.shape[1] // HEAD
    group_size = w_query.shape[1] // (HEAD * kv_local)
    normed = rms_norm(hidden, norm_gain)
    cos_t, sin_t = rope_tables(positions)
    q_proj = jnp.dot(normed, w_query, preferred_element_type=jnp.float32).reshape(row_count, kv_local, group_size, HEAD)
    queries = apply_rope(q_proj, cos_t[:, None, None, :], sin_t[:, None, None, :]).astype(jnp.bfloat16)
    k_proj = jnp.dot(normed, w_key, preferred_element_type=jnp.float32).reshape(row_count, kv_local, HEAD)
    k_rope = apply_rope(k_proj, cos_t[:, None, :], sin_t[:, None, :]).astype(jnp.bfloat16)
    v_heads = jnp.dot(normed, w_value, preferred_element_type=jnp.float32).astype(jnp.bfloat16).reshape(row_count, kv_local, HEAD)
    return queries, k_rope, v_heads


def own_block_stats(queries, k_rope, v_heads, positions):
    scores = jnp.einsum('uohf,tof->ohut', queries, k_rope, preferred_element_type=jnp.float32) * SCORE_SCALE
    visible = positions[None, :] <= positions[:, None]
    scores = jnp.where(visible, scores, -jnp.inf)
    run_max = jnp.max(scores, axis=-1)
    weights = jnp.exp(scores - run_max[..., None])
    run_sum = jnp.sum(weights, axis=-1)
    acc_out = jnp.einsum('ohut,tof->ohuf', weights.astype(jnp.bfloat16), v_heads, preferred_element_type=jnp.float32)
    return run_max, run_sum, acc_out


def attend_block(queries, kv_blk, soft_stats):
    run_max, run_sum, acc_out = soft_stats
    scores = jnp.einsum('uohf,tof->ohut', queries, kv_blk[0], preferred_element_type=jnp.float32) * SCORE_SCALE
    new_max = jnp.maximum(run_max, jnp.max(scores, axis=-1))
    rescale = jnp.exp(run_max - new_max)
    weights = jnp.exp(scores - new_max[..., None])
    new_sum = run_sum * rescale + jnp.sum(weights, axis=-1)
    new_acc = acc_out * rescale[..., None] + jnp.einsum('ohut,tof->ohuf', weights.astype(jnp.bfloat16), kv_blk[1], preferred_element_type=jnp.float32)
    return new_max, new_sum, new_acc


def output_sum(hidden, soft_stats, w_out):
    run_max, run_sum, acc_out = soft_stats
    attn_o = (acc_out / run_sum[..., None]).astype(jnp.bfloat16)
    w_out_r = w_out.reshape(acc_out.shape[0], acc_out.shape[1], HEAD, hidden.shape[1])
    part_sum = jnp.einsum('ngte,ngef->tf', attn_o, w_out_r, preferred_element_type=jnp.float32).astype(jnp.bfloat16)
    attn_sum = lax.psum(part_sum, 'tp')
    return (hidden.astype(jnp.float32) + attn_sum.astype(jnp.float32)).astype(jnp.bfloat16)


def solution(mesh):
    blocks = mesh.shape['cp']
    shift_pairs = [(src_idx, (src_idx + 1) % blocks) for src_idx in range(blocks)]
    row_spec = P(('dp', 'cp'), None)
    cache_spec = P(('dp', 'cp'), 'tp', None)
    head_cols = P(None, 'tp')

    def local_block(hidden, positions, norm_gain, w_query, w_key, w_value, w_out):
        my_block = lax.axis_index('cp')
        queries, k_rope, v_heads = project_heads(hidden, positions, norm_gain, w_query, w_key, w_value)
        soft_stats = own_block_stats(queries, k_rope, v_heads, positions)

        def shift_step(step_idx, loop_carry):
            kv_blk, stats_in = loop_carry
            kv_blk = lax.ppermute(kv_blk, 'cp', shift_pairs)

            def take_block(state_in):
                return attend_block(queries, kv_blk, state_in)

            def keep_stats(state_in):
                return state_in

            stats_out = lax.cond(step_idx <= my_block, take_block, keep_stats, stats_in)
            return kv_blk, stats_out

        kv_own = jnp.stack([k_rope, v_heads])
        _, soft_stats = lax.fori_loop(1, blocks, shift_step, (kv_own, soft_stats))
        return output_sum(hidden, soft_stats, w_out), k_rope, v_heads

    return jax.shard_map(local_block, mesh=mesh, in_specs=(row_spec, P(('dp', 'cp')), P(None), head_cols, head_cols, head_cols, P('tp', None)), out_specs=(row_spec, cache_spec, cache_spec), check_vma=False)
```

profile of v0, /device:TPU:7, one launch (start us, length us, event | category | flops | bytes accessed | tf_op | source)
XLA Modules:
  0.0 527.5 jit_solution(4253180510917700517)
XLA Ops:
  8.1 1.0 broadcast_compare_fusion
  9.1 1.1 convert_element_type.51
  10.2 5.1 fusion.17
  15.3 5.1 fusion.36
  20.9 24.2 %convolution_bitcast_fusion = f32[64,8,16,128]{3,1,2,0:T(8,128)S(1)} fusion(bf16[8192,2048]{1,0:T(8,128)(2,1)} %param.14, bf16[512,8192]{1,0:T(8,128)(2,1)} %param.11, f32[8192]{0:T(1024)S(1)} %convert_element_type.51, f32[512]{0:T(512)S(1)} %add_rsqrt_fusion), kind=kOutput, calls=%fused_computation.37 | convolution fusion | flops 17196646400 | bytes 46172160 | tf_op jit(solution)/shard_map/dot_general | solution.py:39
  46.0 3.4 fusion.38
  49.4 5.1 convolution_convert_fusion
  54.5 1.0 multiply_cosine_fusion
  55.8 5.7 %subtract_convert_fusion = (bf16[512,2,8,64]{3,0,2,1:T(8,128)(2,1)S(1)}, bf16[512,2,8,64]{3,0,2,1:T(8,128)(2,1)S(1)}) fusion(f32[512,2,8,64]{3,2,1,0:T(8,128)} %get-tuple-element.184, f32[512,2,8,64]{3,2,1,0:T(8,128)S(1)} %get-tuple-element.183, f32[512,64]{1,0:T(8,128)S(1)} %get-tuple-element.190, f32[512,64]{1,0:T(8,128)S(1)} %get-tuple-element.189), kind=kLoop, calls=%fused_computation.36 | loop fusion | flops 4194304 | bytes 6553600 | tf_op jit(solution)/shard_map/convert
  61.5 1.2 pad_maximum_fusion
  62.6 7.4 %fusion.25 = (f32[2,8,512]{2,1,0:T(8,128)S(1)}, f32[2,512,512,8]{2,1,3,0:T(8,128)}) fusion(pred[512,512]{0,1:T(8,128)(4,1)S(1)} %broadcast_compare_fusion, bf16[512,2,8,128]{3,0,2,1:T(8,128)(2,1)S(1)} %pad_maximum_fusion, bf16[512,2,128]{2,0,1:T(8,128)(2,1)S(1)} %pad_maximum_fusion.2), kind=kOutput, calls=%fused_computation.31 | convolution fusion | flops 1086316544 | bytes 19431424 | tf_op jit(solution)/shard_map/uohf,tof->ohut/dot_general | solution.py:48
  70.0 9.1 %fusion.22 = f32[2,8,512]{2,1,0:T(8,128)S(1)} fusion(f32[2,512,512,8]{2,1,3,0:T(8,128)} %get-tuple-element.192, f32[2,8,512]{2,1,0:T(8,128)S(1)} %get-tuple-element.250, pred[512,512]{0,1:T(8,128)(4,1)S(1)} %broadcast_compare_fusion), kind=kLoop, calls=%fused_computation.30 | loop fusion | flops 16769024 | bytes 17104896 | tf_op jit(solution)/shard_map/reduce_sum | solution.py:53
  79.2 12.7 %fusion.26 = f32[2,8,512,128]{3,2,1,0:T(8,128)} fusion(bf16[512,2,128,1]{0,2,3,1:T(8,128)(2,1)S(1)} %bitcast.71, f32[2,512,512,8]{2,1,3,0:T(8,128)} %get-tuple-element.192, f32[2,8,512]{2,1,0:T(8,128)S(1)} %get-tuple-element.250, pred[512,512]{0,1:T(8,128)(4,1)S(1)} %broadcast_compare_fusion), kind=kOutput, calls=%fused_computation.32 | convolution fusion | flops 1090519040 | bytes 21528576 | tf_op jit(solution)/shard_map/ohut,tof->ohuf/dot_general | solution.py:54
  93.0 104.3 %while.19 = (s32[]{:T(128)}, bf16[2,512,2,128]{3,1,2,0:T(8,128)(2,1)}, f32[2,8,512]{2,1,0:T(8,128)S(1)}, f32[2,8,512]{2,1,0:T(8,128)S(1)}, f32[2,8,512,128]{3,2,...) while((s32[]{:T(128)}, bf16[2,512,2,128]{3,1,2,0:T(8,128)(2,1)}, ...), condition=%wide.region_8.9_spmd, body=%wide.region_3.8_spmd.sunk | while | flops 2183151616 | bytes 65011944 | solution.py:104
  94.1 6.1 %collective-permute-done = bf16[2,512,2,128]{3,1,2,0:T(8,128)(2,1)S(1)} collective-permute-done((bf16[2,512,2,128]{3,1,2,0:T(8,128)(2,1)}, bf16[2,512,2,128]{3,1,2,0:T(8,128)(2,1)S(1)}, u32[]{:S(2)}, u32[]{:S(2)}) %collective-permute-start) | collective-permute-done | bytes 524320 | tf_op jit(solution)/shard_map/while/body/eval_jaxpr/ppermute | solution.py:92
  100.2 27.4 %conditional.2 = ((f32[2,8,512]{2,1,0:T(8,128)S(1)}, f32[2,8,512]{2,1,0:T(8,128)S(1)}, f32[2,8,512,128]{3,2,1,0:T(8,128)})) conditional(s32[]{:T(128)} %convert_element_type.92, (f32[2,8,512]{2,1,0:T(8,128)S(1)}, f32[2,8,512]{2,1,0:T(8,128)S(1)}, f32[2,8,512,128]{3,2,1,0:T(8,128)}) %tuple.50, (bf16[2,512,2,128]{3,1,2,0:T(8,128)(2,1)S(1)}, ...), branch_computations={%region_4.4_spmd, %region_5.7_spmd} | conditional | flops 2183151616 | bytes 61866016 | solution.py:100
  100.2 8.1 %bitcast_reduce_fusion = (f32[2,8,512]{2,1,0:T(8,128)S(1)}, f32[2,512,512,8]{2,1,3,0:T(8,128)}) fusion(bf16[512,2,8,128]{3,0,2,1:T(8,128)(2,1)S(1)} %get-tuple-element.139, bf16[2,512,2,128]{3,1,2,0:T(8,128)(2,1)S(1)} %get-tuple-element.138), kind=kOutput, calls=%fused_computation.1 | convolution fusion | flops 1082122240 | bytes 19169280 | tf_op jit(solution)/shard_map/while/body/eval_jaxpr/cond/branch_1_fun/uohf,tof->ohut/dot_general | solution.py:60
  108.3 8.6 %fusion.2 = f32[2,8,512]{2,1,0:T(8,128)S(1)} fusion(f32[2,512,512,8]{2,1,3,0:T(8,128)} %get-tuple-element.180, f32[2,8,512]{2,1,0:T(8,128)S(1)} %max.2), kind=kLoop, calls=%fused_computation.4 | loop fusion | flops 12574720 | bytes 16842752 | tf_op jit(solution)/shard_map/while/body/eval_jaxpr/cond/branch_1_fun/reduce_sum | solution.py:64
  116.9 10.8 %multiply_add_fusion = f32[2,8,512,128]{3,2,1,0:T(8,128)} fusion(f32[2,8,512,128]{3,2,1,0:T(8,128)} %get-tuple-element.141, f32[2,8,512]{2,1,0:T(8,128)S(1)} %get-tuple-element.178, f32[2,512,512,8]{2,1,3,0:T(8,128)} %get-tuple-element.180, f32[2,8,512]{2,1,0:T(8,128)S(1)} %max.2, bf16[2,512,2,128]{3,1,2,0:T(8,128)(2,1)S(1)} %get-tuple-element.138), kind=kOutput, calls=%fused_computation.8 | convolution fusion | flops 1088421888 | bytes 25493504 | tf_op jit(solution)/shard_map/while/body/eval_jaxpr/cond/branch_1_fun/ohut,tof->ohuf/dot_general | solution.py:65
  128.4 6.1 %collective-permute-done = bf16[2,512,2,128]{3,1,2,0:T(8,128)(2,1)S(1)} collective-permute-done((bf16[2,512,2,128]{3,1,2,0:T(8,128)(2,1)}, bf16[2,512,2,128]{3,1,2,0:T(8,128)(2,1)S(1)}, u32[]{:S(2)}, u32[]{:S(2)}) %collective-permute-start) | collective-permute-done | bytes 524320 | tf_op jit(solution)/shard_map/while/body/eval_jaxpr/ppermute | solution.py:92
  134.5 27.4 %conditional.2 = ((f32[2,8,512]{2,1,0:T(8,128)S(1)}, f32[2,8,512]{2,1,0:T(8,128)S(1)}, f32[2,8,512,128]{3,2,1,0:T(8,128)})) conditional(s32[]{:T(128)} %convert_element_type.92, (f32[2,8,512]{2,1,0:T(8,128)S(1)}, f32[2,8,512]{2,1,0:T(8,128)S(1)}, f32[2,8,512,128]{3,2,1,0:T(8,128)}) %tuple.50, (bf16[2,512,2,128]{3,1,2,0:T(8,128)(2,1)S(1)}, ...), branch_computations={%region_4.4_spmd, %region_5.7_spmd} | conditional | flops 2183151616 | bytes 61866016 | solution.py:100
  134.5 8.1 %bitcast_reduce_fusion = (f32[2,8,512]{2,1,0:T(8,128)S(1)}, f32[2,512,512,8]{2,1,3,0:T(8,128)}) fusion(bf16[512,2,8,128]{3,0,2,1:T(8,128)(2,1)S(1)} %get-tuple-element.139, bf16[2,512,2,128]{3,1,2,0:T(8,128)(2,1)S(1)} %get-tuple-element.138), kind=kOutput, calls=%fused_computation.1 | convolution fusion | flops 1082122240 | bytes 19169280 | tf_op jit(solution)/shard_map/while/body/eval_jaxpr/cond/branch_1_fun/uohf,tof->ohut/dot_general | solution.py:60
  142.6 8.6 %fusion.2 = f32[2,8,512]{2,1,0:T(8,128)S(1)} fusion(f32[2,512,512,8]{2,1,3,0:T(8,128)} %get-tuple-element.180, f32[2,8,512]{2,1,0:T(8,128)S(1)} %max.2), kind=kLoop, calls=%fused_computation.4 | loop fusion | flops 12574720 | bytes 16842752 | tf_op jit(solution)/shard_map/while/body/eval_jaxpr/cond/branch_1_fun/reduce_sum | solution.py:64
  151.2 10.8 %multiply_add_fusion = f32[2,8,512,128]{3,2,1,0:T(8,128)} fusion(f32[2,8,512,128]{3,2,1,0:T(8,128)} %get-tuple-element.141, f32[2,8,512]{2,1,0:T(8,128)S(1)} %get-tuple-element.178, f32[2,512,512,8]{2,1,3,0:T(8,128)} %get-tuple-element.180, f32[2,8,512]{2,1,0:T(8,128)S(1)} %max.2, bf16[2,512,2,128]{3,1,2,0:T(8,128)(2,1)S(1)} %get-tuple-element.138), kind=kOutput, calls=%fused_computation.8 | convolution fusion | flops 1088421888 | bytes 25493504 | tf_op jit(solution)/shard_map/while/body/eval_jaxpr/cond/branch_1_fun/ohut,tof->ohuf/dot_general | solution.py:65
  162.8 6.3 %collective-permute-done = bf16[2,512,2,128]{3,1,2,0:T(8,128)(2,1)S(1)} collective-permute-done((bf16[2,512,2,128]{3,1,2,0:T(8,128)(2,1)}, bf16[2,512,2,128]{3,1,2,0:T(8,128)(2,1)S(1)}, u32[]{:S(2)}, u32[]{:S(2)}) %collective-permute-start) | collective-permute-done | bytes 524320 | tf_op jit(solution)/shard_map/while/body/eval_jaxpr/ppermute | solution.py:92
  169.1 27.4 %conditional.2 = ((f32[2,8,512]{2,1,0:T(8,128)S(1)}, f32[2,8,512]{2,1,0:T(8,128)S(1)}, f32[2,8,512,128]{3,2,1,0:T(8,128)})) conditional(s32[]{:T(128)} %convert_element_type.92, (f32[2,8,512]{2,1,0:T(8,128)S(1)}, f32[2,8,512]{2,1,0:T(8,128)S(1)}, f32[2,8,512,128]{3,2,1,0:T(8,128)}) %tuple.50, (bf16[2,512,2,128]{3,1,2,0:T(8,128)(2,1)S(1)}, ...), branch_computations={%region_4.4_spmd, %region_5.7_spmd} | conditional | flops 2183151616 | bytes 61866016 | solution.py:100
  169.1 8.1 %bitcast_reduce_fusion = (f32[2,8,512]{2,1,0:T(8,128)S(1)}, f32[2,512,512,8]{2,1,3,0:T(8,128)}) fusion(bf16[512,2,8,128]{3,0,2,1:T(8,128)(2,1)S(1)} %get-tuple-element.139, bf16[2,512,2,128]{3,1,2,0:T(8,128)(2,1)S(1)} %get-tuple-element.138), kind=kOutput, calls=%fused_computation.1 | convolution fusion | flops 1082122240 | bytes 19169280 | tf_op jit(solution)/shard_map/while/body/eval_jaxpr/cond/branch_1_fun/uohf,tof->ohut/dot_general | solution.py:60
  177.2 8.6 %fusion.2 = f32[2,8,512]{2,1,0:T(8,128)S(1)} fusion(f32[2,512,512,8]{2,1,3,0:T(8,128)} %get-tuple-element.180, f32[2,8,512]{2,1,0:T(8,128)S(1)} %max.2), kind=kLoop, calls=%fused_computation.4 | loop fusion | flops 12574720 | bytes 16842752 | tf_op jit(solution)/shard_map/while/body/eval_jaxpr/cond/branch_1_fun/reduce_sum | solution.py:64
  185.8 10.8 %multiply_add_fusion = f32[2,8,512,128]{3,2,1,0:T(8,128)} fusion(f32[2,8,512,128]{3,2,1,0:T(8,128)} %get-tuple-element.141, f32[2,8,512]{2,1,0:T(8,128)S(1)} %get-tuple-element.178, f32[2,512,512,8]{2,1,3,0:T(8,128)} %get-tuple-element.180, f32[2,8,512]{2,1,0:T(8,128)S(1)} %max.2, bf16[2,512,2,128]{3,1,2,0:T(8,128)(2,1)S(1)} %get-tuple-element.138), kind=kOutput, calls=%fused_computation.8 | convolution fusion | flops 1088421888 | bytes 25493504 | tf_op jit(solution)/shard_map/while/body/eval_jaxpr/cond/branch_1_fun/ohut,tof->ohuf/dot_general | solution.py:65
  197.3 24.2 %bitcast_convert_fusion = bf16[512,8192]{1,0:T(8,128)(2,1)} fusion(bf16[2,8,128,8192]{3,2,1,0:T(8,128)(2,1)} %bitcast.75, f32[2,8,512,128]{3,2,1,0:T(8,128)} %get-tuple-element.158, f32[2,8,512]{2,1,0:T(8,128)S(1)} %get-tuple-element.159), kind=kOutput, calls=%fused_computation.26 | convolution fusion | flops 17186160640 | bytes 46170112 | tf_op jit(solution)/shard_map/ngte,ngef->tf/dot_general | solution.py:73
  223.4 287.3 %all-reduce.2.cloned.1.call-done = bf16[512,8192]{1,0:T(8,128)(2,1)} async-done(((bf16[512,8192]{1,0:T(8,128)(2,1)}), bf16[512,8192]{1,0:T(8,128)(2,1)}) %all-reduce.2.cloned.1.call-update) | async-done | bytes 8388624 | tf_op jit(solution)/shard_map/psum | solution.py:74
  510.7 9.5 %fusion.20 = bf16[512,8192]{1,0:T(8,128)(2,1)} fusion(bf16[512,8192]{1,0:T(8,128)(2,1)} %param.11, bf16[512,8192]{1,0:T(8,128)(2,1)} %all-reduce.2.cloned.1.call-done), kind=kLoop, calls=%fused_computation.25 | loop fusion | flops 16777216 | bytes 25165824 | tf_op jit(solution)/shard_map/convert_element_type | solution.py:75
  (37 shorter events, 8.9 us)
Async XLA Ops:
  7.2 503.6 %all-reduce.2.cloned.1.call-start = ((), (), s32[]{:S(2)}) async-start(), calls=%async_computation | async-start | bytes 16777216 | tf_op jit(solution)/shard_map/psum | solution.py:74
  7.2 8.1 %copy-start = (bf16[512,8192]{1,0:T(8,128)(2,1)S(1)}, bf16[512,8192]{1,0:T(8,128)(2,1)}, u32[]{:S(2)}) copy-start(bf16[512,8192]{1,0:T(8,128)(2,1)} %param.11) | copy-start | bytes 25165828
  45.0 4.4 slice-start
  46.0 3.4 slice-start.1
  93.3 6.9 %collective-permute-start = (bf16[2,512,2,128]{3,1,2,0:T(8,128)(2,1)}, bf16[2,512,2,128]{3,1,2,0:T(8,128)(2,1)S(1)}, u32[]{:S(2)}, u32[]{:S(2)}) collective-permute-start(bf16[2,512,2,128]{3,1,2,0:T(8,128)(2,1)} %get-tuple-element.257), channel_id=1, source_target_pairs={{0,1},{1,2},{2,3},{3,0},{4,5},{5,6},{6,7},{7,4},{8,9},{9,10},{10,1... | collective-permute-start | bytes 1572872 | tf_op jit(solution)/shard_map/while/body/eval_jaxpr/ppermute | solution.py:92
  128.4 6.1 %collective-permute-start = (bf16[2,512,2,128]{3,1,2,0:T(8,128)(2,1)}, bf16[2,512,2,128]{3,1,2,0:T(8,128)(2,1)S(1)}, u32[]{:S(2)}, u32[]{:S(2)}) collective-permute-start(bf16[2,512,2,128]{3,1,2,0:T(8,128)(2,1)} %get-tuple-element.257), channel_id=1, source_target_pairs={{0,1},{1,2},{2,3},{3,0},{4,5},{5,6},{6,7},{7,4},{8,9},{9,10},{10,1... | collective-permute-start | bytes 1572872 | tf_op jit(solution)/shard_map/while/body/eval_jaxpr/ppermute | solution.py:92
  162.8 6.3 %collective-permute-start = (bf16[2,512,2,128]{3,1,2,0:T(8,128)(2,1)}, bf16[2,512,2,128]{3,1,2,0:T(8,128)(2,1)S(1)}, u32[]{:S(2)}, u32[]{:S(2)}) collective-permute-start(bf16[2,512,2,128]{3,1,2,0:T(8,128)(2,1)} %get-tuple-element.257), channel_id=1, source_target_pairs={{0,1},{1,2},{2,3},{3,0},{4,5},{5,6},{6,7},{7,4},{8,9},{9,10},{10,1... | collective-permute-start | bytes 1572872 | tf_op jit(solution)/shard_map/while/body/eval_jaxpr/ppermute | solution.py:92
Sparse Core Ops, SparseCore 0:
  221.7 288.9 all-reduce.1
where the time goes:
time: 536 us; the launch traced here: 527 us
  waiting for transfers between devices  306 us (57%)
  matrix products  135 us (25%)
  other arithmetic  61.5 us (11%)
  between operations  14.6 us (3%)
  local copies, waits for them, and re-layouts  9.19 us (2%)
    psum x1, waiting for transfers between devices, output_sum(): attn_sum = lax.psum(part_sum, 'tp')  287 us
    dot_general x3, matrix products, attend_block(): jnp.einsum('ohut,tof->ohuf', weights.astype(jnp.bfloat16), kv_blk[1], pre...  32.3 us
    reduce_sum x3, other arithmetic, attend_block(): new_sum = run_sum * rescale + jnp.sum(weights, axis=-1)  25.7 us
    dot_general x3, matrix products, attend_block(): jnp.einsum('uohf,tof->ohut', queries, kv_blk[0], preferred_element_type=j...  24.2 us
    dot_general x1, matrix products, output_sum(): jnp.einsum('ngte,ngef->tf', attn_o, w_out_r, preferred_element_type=jnp.f...  24.2 us
    dot_general x1, matrix products, project_heads(): jnp.dot(normed, w_query, preferred_element_type=jnp.float32)  24.2 us
    ppermute x3, waiting for transfers between devices, shift_step(): kv_blk = lax.ppermute(kv_blk, 'cp', shift_pairs)  18.5 us
    dot_general x1, matrix products, own_block_stats(): jnp.einsum('ohut,tof->ohuf', weights.astype(jnp.bfloat16), v_heads, prefe...  12.7 us
  transfers between devices with their start and end apart: 4, of which 4 were waited for; matrix products, arithmetic and copies ran while one was open for 0% of the time, Pallas kernels for 0%

commit v1 on v0

v1 whole, which is shorter than its diff:
```python
import functools
import math
import jax
import jax.numpy as jnp
from jax import lax
from jax.experimental import pallas as pl
from jax.experimental.pallas import tpu as pltpu
from jax.sharding import PartitionSpec as P

HEAD = 128
EPS = 1e-5
LOG_THETA = math.log(1000000.0)
EXP2_SCALE = math.log2(math.e) / math.sqrt(HEAD)
MESH = pl.DeviceIdType.MESH
BLOCKS = 4
COLS = 1024
TILE = 256
RING = 4


def rope_tables(positions):
    half_dim = HEAD // 2
    inv_freq = jnp.exp(jnp.arange(half_dim, dtype=jnp.float32) * (-2.0 * LOG_THETA / HEAD))
    angles = positions.astype(jnp.float32)[..., None] * inv_freq
    cos_t, sin_t = jnp.cos(angles), jnp.sin(angles)
    return jnp.concatenate([cos_t, cos_t], axis=-1), jnp.concatenate([-sin_t, sin_t], axis=-1)


def block_kernel(hidden, gain, cos_ref, sin_ref, w_query, w_key, w_value, w_out,
                 out_ref, kv_out,
                 xbuf, hbuf, wbuf, qbuf, kvbuf, obuf, acc, part, buf_a, buf_b,
                 xsem, wsem, kv_send, kv_recv, kv_osem, send_a, recv_a, send_b, recv_b, out_sem):
    rows, width = xbuf.shape
    q_tiles = qbuf.shape[0]
    depth = wbuf.shape[2]
    br = rows // BLOCKS
    chunks = width // COLS
    group = q_tiles
    ticks = BLOCKS * chunks
    cp = lax.axis_index("cp")
    tp = lax.axis_index("tp")
    is_outer = jnp.logical_or(tp == 0, tp == 3)
    is_inner = jnp.logical_not(is_outer)

    def x_copy(b):
        sl = pl.ds(b * br, br)
        return pltpu.make_async_copy(hidden.at[sl, :], xbuf.at[sl, :], xsem.at[b])

    def col_tile(w_ref, col, slot, piece):
        return pltpu.make_async_copy(w_ref.at[pl.ds(piece * depth, depth), pl.ds(col, TILE)],
                                     wbuf.at[slot, piece], wsem.at[slot, piece])

    def out_tile(col, slot, piece):
        return pltpu.make_async_copy(w_out.at[:, pl.ds(col + piece * TILE, TILE)],
                                     wbuf.at[slot, piece], wsem.at[slot, piece])

    def start_key():
        for piece in range(4):
            col_tile(w_key, 0, 0, piece).start()

    def start_value():
        for piece in range(4):
            col_tile(w_value, 0, 1, piece).start()

    def start_query(j):
        for piece in range(4):
            col_tile(w_query, pl.multiple_of(j * TILE, TILE), lax.rem(j + 2, RING), piece).start()

    def start_out(t):
        col = pl.multiple_of(lax.rem(t, chunks) * COLS, COLS)
        for piece in range(4):
            out_tile(col, lax.rem(t + 2 + q_tiles, RING), piece).start()

    for b in range(BLOCKS):
        x_copy(b).start()
    start_key()

    barrier = pltpu.get_barrier_semaphore()
    for peer in ({"cp": cp ^ 1}, {"cp": cp ^ 2}, {"tp": tp ^ 1}, {"tp": 3 - tp}):
        pl.semaphore_signal(barrier, inc=1, device_id=peer, device_id_type=MESH)

    for b in range(BLOCKS):
        x_copy(b).wait()
        if b == 0:
            start_value()
        elif b <= 2:
            start_query(b - 1)

        def norm_rows(i, carry):
            sl = pl.ds(pl.multiple_of(b * br + i * 16, 16), 16)
            xf = xbuf[sl, :].astype(jnp.float32)
            inv = lax.rsqrt(jnp.mean(xf * xf, axis=-1, keepdims=True) + EPS)
            hbuf[sl, :] = (xf * inv * gain[...].astype(jnp.float32)).astype(jnp.bfloat16)
            return carry

        lax.fori_loop(0, br // 16, norm_rows, 0)

    def project(slot, copy_of):
        def piece_step(piece, carry):
            copy_of(piece).wait()
            prod = jnp.dot(hbuf[:, pl.ds(pl.multiple_of(piece * depth, depth), depth)], wbuf[slot, piece],
                           preferred_element_type=jnp.float32)

            @pl.when(piece == 0)
            def _():
                acc[...] = prod

            @pl.when(piece > 0)
            def _():
                acc[...] += prod

            return carry

        lax.fori_loop(0, 4, piece_step, 0)

    def roped(head):
        vals = acc[:, head * HEAD:(head + 1) * HEAD]
        return (vals * cos_ref[...] + pltpu.roll(vals, HEAD // 2, 1) * sin_ref[...]).astype(jnp.bfloat16)

    project(0, lambda piece: col_tile(w_key, 0, 0, piece))
    start_query(2) if q_tiles > 2 else start_out(2 - q_tiles)
    for head in range(2):
        kvbuf[cp, head] = roped(head)
    project(1, lambda piece: col_tile(w_value, 0, 1, piece))
    start_query(3) if q_tiles > 3 else start_out(3 - q_tiles)
    for head in range(2):
        kvbuf[cp, 2 + head] = acc[:, head * HEAD:(head + 1) * HEAD].astype(jnp.bfloat16)

    pl.semaphore_wait(barrier, 4)

    def kv_copy(slot, sem, target):
        return pltpu.make_async_remote_copy(src_ref=kvbuf.at[slot], dst_ref=kvbuf.at[slot],
                                            send_sem=kv_send.at[sem], recv_sem=kv_recv.at[slot],
                                            device_id={"cp": target}, device_id_type=MESH)

    def cache_copy():
        return pltpu.make_async_copy(kvbuf.at[cp], kv_out, kv_osem)

    @pl.when(cp == 0)
    def _():
        kv_copy(0, 0, 2).start()
        kv_copy(0, 1, 1).start()

    @pl.when(cp == 1)
    def _():
        kv_copy(1, 0, 3).start()

    @pl.when(cp == 2)
    def _():
        kv_copy(2, 0, 3).start()

    cache_copy().start()

    relay_at = max(q_tiles - 2, 0)

    def query_step(j, carry):
        slot = lax.rem(j + 2, RING)
        project(slot, lambda piece: col_tile(w_query, pl.multiple_of(j * TILE, TILE), slot, piece))

        @pl.when(j + RING < q_tiles)
        def _():
            start_query(j + RING)

        @pl.when(j + RING >= q_tiles)
        def _():
            start_out(j + RING - q_tiles)

        for head in range(2):
            qbuf[j, head] = roped(head)

        @pl.when(jnp.logical_and(j == relay_at, cp == 2))
        def _():
            kv_copy(0, 1, 3).wait_recv()
            kv_copy(0, 1, 3).start()

        @pl.when(jnp.logical_and(j == relay_at, cp == 3))
        def _():
            kv_copy(1, 1, 2).wait_recv()
            kv_copy(1, 1, 2).start()

        return carry

    lax.fori_loop(0, q_tiles, query_step, 0)

    @pl.when(cp == 1)
    def _():
        kv_copy(0, 0, 0).wait_recv()

    @pl.when(cp == 2)
    def _():
        kv_copy(1, 0, 0).wait_recv()

    @pl.when(cp == 3)
    def _():
        kv_copy(2, 0, 0).wait_recv()
        kv_copy(0, 0, 0).wait_recv()

    def attend(b, j):
        kv_head = lax.div(2 * j, group)
        qs = qbuf[j, :, pl.ds(pl.multiple_of(b * br, br), br), :].reshape(2 * br, HEAD)

        def scores_of(slot):
            return lax.dot_general(qs, kvbuf[slot, kv_head], (((1,), (1,)), ((), ())),
                                   preferred_element_type=jnp.float32)

        scores = scores_of(cp)
        row = lax.broadcasted_iota(jnp.int32, scores.shape, 0) % br + b * br
        key = lax.broadcasted_iota(jnp.int32, scores.shape, 1)
        scores = jnp.where(key <= row, scores, -jnp.inf)
        top = jnp.max(scores, axis=-1, keepdims=True)
        probs = jnp.exp2((scores - top) * EXP2_SCALE)
        total = jnp.sum(probs, axis=-1, keepdims=True)
        mixed = jnp.dot(probs.astype(jnp.bfloat16), kvbuf[cp, 2 + kv_head], preferred_element_type=jnp.float32)

        def earlier(slot, carry):
            top, total, mixed = carry
            scores = scores_of(slot)
            new_top = jnp.maximum(top, jnp.max(scores, axis=-1, keepdims=True))
            fade = jnp.exp2((top - new_top) * EXP2_SCALE)
            probs = jnp.exp2((scores - new_top) * EXP2_SCALE)
            total = total * fade + jnp.sum(probs, axis=-1, keepdims=True)
            mixed = mixed * fade + jnp.dot(probs.astype(jnp.bfloat16), kvbuf[slot, 2 + kv_head],
                                           preferred_element_type=jnp.float32)
            return new_top, total, mixed

        top, total, mixed = lax.fori_loop(0, cp, earlier, (top, total, mixed))
        attn = (mixed / total).astype(jnp.bfloat16)
        obuf[lax.rem(b, 2), j] = jnp.concatenate([attn[:br], attn[br:]], axis=1)

    def first_block(j, carry):
        attend(0, j)
        return carry

    lax.fori_loop(0, q_tiles, first_block, 0)

    def chunk(ref, t):
        b, j = lax.div(t, chunks), lax.rem(t, chunks)
        return ref.at[pl.ds(pl.multiple_of(b * br, br), br), pl.ds(pl.multiple_of(j * COLS, COLS), COLS)]

    def partial_copy(t):
        return pltpu.make_async_remote_copy(src_ref=chunk(buf_a, t), dst_ref=chunk(buf_a, t),
                                            send_sem=send_a.at[t], recv_sem=recv_a.at[t],
                                            device_id={"tp": tp ^ 1}, device_id_type=MESH)

    def pair_copy(t):
        return pltpu.make_async_remote_copy(src_ref=chunk(buf_a, t), dst_ref=chunk(buf_b, t),
                                            send_sem=send_a.at[t], recv_sem=recv_b.at[t],
                                            device_id={"tp": 3 - tp}, device_id_type=MESH)

    def final_copy(t):
        return pltpu.make_async_remote_copy(src_ref=chunk(buf_b, t), dst_ref=chunk(buf_b, t),
                                            send_sem=send_b.at[t], recv_sem=recv_b.at[t],
                                            device_id={"tp": tp ^ 1}, device_id_type=MESH)

    def store_copy(t):
        return pltpu.make_async_copy(chunk(buf_b, t), chunk(out_ref, t), out_sem.at[t])

    def finish(t):
        pair_copy(t).wait_recv()
        mine, theirs, res = chunk(buf_a, t), chunk(buf_b, t), chunk(xbuf, t)
        attn_sum = mine[...].astype(jnp.float32) + theirs[...].astype(jnp.float32)
        theirs[...] = (res[...].astype(jnp.float32) + attn_sum).astype(jnp.bfloat16)
        final_copy(t).start()
        store_copy(t).start()

    def tick(t, carry):
        b, j = lax.div(t, chunks), lax.rem(t, chunks)
        slot = lax.rem(t + 2 + q_tiles, RING)
        col = pl.multiple_of(j * COLS, COLS)
        for piece in range(4):
            out_tile(col, slot, piece).wait()
        lhs = jnp.concatenate([obuf[lax.rem(b, 2), i] for i in range(q_tiles)], axis=1)
        for piece in range(4):
            part[:, piece * TILE:(piece + 1) * TILE] = jnp.dot(lhs, wbuf[slot, piece],
                                                              preferred_element_type=jnp.float32)

        @pl.when(t + RING < ticks)
        def _():
            start_out(t + RING)

        @pl.when(is_outer)
        def _():
            chunk(buf_a, t)[...] = part[...].astype(jnp.bfloat16)
            partial_copy(t).start()

        @pl.when(jnp.logical_and(is_inner, t >= 2))
        def _():
            finish(t - 2)

        @pl.when(b + 1 < BLOCKS)
        def _():
            attend(b + 1, j)

        @pl.when(is_inner)
        def _():
            partial_copy(t).wait_recv()
            mine = chunk(buf_a, t)
            mine[...] = (part[...] + mine[...].astype(jnp.float32)).astype(jnp.bfloat16)
            pair_copy(t).start()

        return carry

    lax.fori_loop(0, ticks, tick, 0)

    @pl.when(is_inner)
    def _():
        finish(ticks - 2)
        finish(ticks - 1)

        def drain(t, carry):
            pair_copy(t).wait_send()
            final_copy(t).wait_send()
            store_copy(t).wait()
            return carry

        lax.fori_loop(0, ticks, drain, 0)

    @pl.when(is_outer)
    def _():
        def arrive(t, carry):
            final_copy(t).wait_recv()
            store_copy(t).start()
            return carry

        lax.fori_loop(0, ticks, arrive, 0)

        def drain(t, carry):
            partial_copy(t).wait_send()
            store_copy(t).wait()
            return carry

        lax.fori_loop(0, ticks, drain, 0)

    @pl.when(cp == 0)
    def _():
        kv_copy(0, 0, 2).wait_send()
        kv_copy(0, 1, 1).wait_send()

    @pl.when(cp == 1)
    def _():
        kv_copy(1, 0, 3).wait_send()

    @pl.when(cp == 2)
    def _():
        kv_copy(2, 0, 3).wait_send()
        kv_copy(0, 1, 3).wait_send()

    @pl.when(cp == 3)
    def _():
        kv_copy(1, 1, 2).wait_send()

    cache_copy().wait()


def solution(mesh):
    row_spec = P(('dp', 'cp'), None)
    cache_spec = P(('dp', 'cp'), 'tp', None)
    head_cols = P(None, 'tp')

    def local_block(hidden, positions, norm_gain, w_query, w_key, w_value, w_out):
        rows, width = hidden.shape
        depth = w_query.shape[1]
        q_tiles = depth // TILE
        kv_cols = w_key.shape[1]
        br = rows // BLOCKS
        ticks = BLOCKS * (width // COLS)
        cos_t, sin_t = rope_tables(positions)
        any_spec = pl.BlockSpec(memory_space=pl.ANY)
        vmem_spec = pl.BlockSpec(memory_space=pltpu.VMEM)
        bf16, f32 = jnp.bfloat16, jnp.float32
        dma = pltpu.SemaphoreType.DMA
        out, kv = pl.pallas_call(
            block_kernel,
            out_shape=(jax.ShapeDtypeStruct((rows, width), bf16),
                       jax.ShapeDtypeStruct((4, rows, HEAD), bf16)),
            in_specs=[any_spec, vmem_spec, vmem_spec, vmem_spec, any_spec, any_spec, any_spec, any_spec],
            out_specs=(any_spec, any_spec),
            scratch_shapes=[
                pltpu.VMEM((rows, width), bf16),
                pltpu.VMEM((rows, width), bf16),
                pltpu.VMEM((RING, 4, depth, TILE), bf16),
                pltpu.VMEM((q_tiles, 2, rows, HEAD), bf16),
                pltpu.VMEM((4, 4, rows, HEAD), bf16),
                pltpu.VMEM((2, q_tiles, br, TILE), bf16),
                pltpu.VMEM((rows, TILE), f32),
                pltpu.VMEM((br, COLS), f32),
                pltpu.VMEM((rows, width), bf16),
                pltpu.VMEM((rows, width), bf16),
                dma((BLOCKS,)), dma((RING, 4)), dma((2,)), dma((4,)), dma,
                dma((ticks,)), dma((ticks,)), dma((ticks,)), dma((ticks,)), dma((ticks,)),
            ],
            compiler_params=pltpu.CompilerParams(collective_id=0, has_side_effects=True,
                                                 vmem_limit_bytes=67043328),
            name="attention_block",
        )(hidden, norm_gain.reshape(1, width), cos_t, sin_t, w_query, w_key, w_value, w_out)
        k_rope = jnp.transpose(kv[:2], (1, 0, 2))
        v_heads = jnp.transpose(kv[2:], (1, 0, 2))
        return out, k_rope, v_heads

    return jax.shard_map(local_block, mesh=mesh, in_specs=(row_spec, P(('dp', 'cp')), P(None), head_cols, head_cols, head_cols, P('tp', None)), out_specs=(row_spec, cache_spec, cache_spec), check_vma=False)
```

time: 536 us -> 272 us (0.51); the launches traced: 527 us -> 272 us
  waiting for transfers between devices: 306 us -> 0 us
  Pallas kernels: 0 us -> 257 us
  matrix products: 135 us -> 0 us
  other arithmetic: 61.5 us -> 2.68 us
  between operations: 14.6 us -> 0.66 us
    psum x1 -> x0, waiting for transfers between devices: 287 us -> none  [output_sum(): attn_sum = lax.psum(part_sum, 'tp')]
    pallas_call x0 -> x1, Pallas kernels: none -> 257 us  [local_block(): pl.pallas_call(block_kernel, out_shape=(jax.ShapeDtypeStruct((rows, width...]
    dot_general x12 -> x0, matrix products: 135 us -> none  [the longest x3 32.3 us: attend_block(): jnp.einsum('ohut,tof->ohuf', weights.astype(jnp.bfloat16), kv_blk[1], pre...]
    reduce_sum x5 -> x0, other arithmetic: 39.9 us -> none  [the longest x3 25.7 us: attend_block(): new_sum = run_sum * rescale + jnp.sum(weights, axis=-1)]
    ppermute x3 -> x0, waiting for transfers between devices: 18.5 us -> none  [shift_step(): kv_blk = lax.ppermute(kv_blk, 'cp', shift_pairs)]
    convert_element_type x2 -> x0, other arithmetic: 10.6 us -> none  [the longest x1 9.49 us: output_sum(): (hidden.astype(jnp.float32) + attn_sum.astype(jnp.float32)).astype(jnp.bf...]
    another operation x3 -> x0, other arithmetic: 6.78 us -> none
    unnamed x11 -> x3, local copies, waits for them, and re-layouts: 3.2 us -> 9.72 us
  transfers between devices with their start and end apart: 4 -> 0, of which waited for: 4 -> 0; matrix products, arithmetic and copies ran while one was open for 0% -> 0% of each run, Pallas kernels for 0% -> 0%
where the time goes in v1:
time: 272 us
  Pallas kernels  257 us (94%)
  local copies, waits for them, and re-layouts  12.1 us (4%)
    pallas_call x1, Pallas kernels, local_block(): pl.pallas_call(block_kernel, out_shape=(jax.ShapeDtypeStruct((rows, width...  257 us
    unnamed x3, local copies, waits for them, and re-layouts  9.72 us

profile of v1, /device:TPU:7, one launch (start us, length us, event | category | flops | bytes accessed | tf_op | source)
XLA Modules:
  0.0 272.2 jit_solution(13468397830922372153)
XLA Ops:
  0.6 0.7 convert_element_type.3
  1.3 1.3 reshape.15.gain
  2.7 1.0 fusion
  3.7 1.0 pad_maximum_fusion
  4.7 256.7 %attention_block.1 = (bf16[512,8192]{1,0:T(8,128)(2,1)}, bf16[4,512,128]{2,1,0:T(8,128)(2,1)}) custom-call(bf16[512,8192]{1,0:T(8,128)(2,1)} %hidden.1, bf16[1,8192]{1,0:T(2,128)(2,1)} %reshape.15.gain, f32[512,128]{1,0:T(8,128)} %get-tuple-element.15.cos_ref, f32[512,128]{1,0:T(8,128)} %get-tuple-element.16.sin_ref, bf16[8192,2048]{1,0:T(8,128)(2,1)} %w_query.1, ...), custom_call_target="tpu_custom_call" | custom-call | tf_op jit(solution)/shard_map/attention_block/pallas_call | solution.py:372
  261.4 1.1 slice_bitcast_fusion
  262.4 1.0 copy.11
  263.4 1.0 copy.10
  264.4 7.8 %copy.13 = bf16[512,8192]{1,0:T(8,128)(2,1)} copy(bf16[512,8192]{1,0:T(8,128)(2,1)} %get-tuple-element.20) | data formatting | bytes 16777216
  (1 shorter events, 0.0 us)

commit v2 on v1

v2 whole, which is shorter than its diff:
```python
import functools
import math
import jax
import jax.numpy as jnp
from jax import lax
from jax.experimental import pallas as pl
from jax.experimental.pallas import tpu as pltpu
from jax.sharding import PartitionSpec as P

HEAD = 128
EPS = 1e-5
LOG_THETA = math.log(1000000.0)
EXP2_SCALE = math.log2(math.e) / math.sqrt(HEAD)
MESH = pl.DeviceIdType.MESH
BLOCKS = 8
PIECES = 4
COLS = 1024
TILE = 256
RING = 4


def rope_table(positions):
    half_dim = HEAD // 2
    lane = jnp.arange(HEAD, dtype=jnp.int32)
    inv_freq = jnp.exp((lane % half_dim).astype(jnp.float32) * (-2.0 * LOG_THETA / HEAD))
    angles = positions.astype(jnp.float32)[..., None] * inv_freq
    return jnp.where(lane < half_dim, jnp.cos(angles), jnp.sin(angles))


def block_kernel(hidden, gain, table, w_query, w_key, w_value, w_out,
                 buf_b, k_out, v_out,
                 xbuf, hbuf, wbuf, w_late, qbuf, kvbuf, obuf, acc, part, buf_a, cos_ref, sin_ref,
                 xsem, wsem, late_sem, kv_send, kv_recv, send_a, recv_a, send_b, recv_b):
    rows, width = xbuf.shape
    q_tiles = qbuf.shape[0]
    depth = wbuf.shape[2]
    br = rows // BLOCKS
    piece_rows = rows // PIECES
    half = rows // 2
    chunks = width // COLS
    group = q_tiles
    ticks = BLOCKS * chunks
    cp = lax.axis_index("cp")
    tp = lax.axis_index("tp")
    is_outer = jnp.logical_or(tp == 0, tp == 3)
    is_inner = jnp.logical_not(is_outer)

    def x_copy(b):
        sl = pl.ds(b * piece_rows, piece_rows)
        return pltpu.make_async_copy(hidden.at[sl, :], xbuf.at[sl, :], xsem.at[b])

    def col_tile(w_ref, col, slot, piece):
        return pltpu.make_async_copy(w_ref.at[pl.ds(piece * depth, depth), pl.ds(col, TILE)],
                                     wbuf.at[slot, piece], wsem.at[slot, piece])

    def late_tile(j, piece):
        return pltpu.make_async_copy(
            w_query.at[pl.ds(piece * depth, depth), pl.ds(pl.multiple_of(j * TILE, TILE), TILE)],
            w_late.at[piece], late_sem.at[piece])

    def out_tile(col, slot, piece):
        return pltpu.make_async_copy(w_out.at[:, pl.ds(col + piece * TILE, TILE)],
                                     wbuf.at[slot, piece], wsem.at[slot, piece])

    def start_key():
        for piece in range(4):
            col_tile(w_key, 0, 0, piece).start()

    def start_value():
        for piece in range(4):
            col_tile(w_value, 0, 1, piece).start()

    def start_query(j):
        for piece in range(4):
            col_tile(w_query, pl.multiple_of(j * TILE, TILE), lax.rem(j + 2, RING), piece).start()

    def start_out(t):
        col = pl.multiple_of(lax.rem(t, chunks) * COLS, COLS)
        for piece in range(4):
            out_tile(col, lax.rem(t + 2 + q_tiles, RING), piece).start()

    for b in range(PIECES):
        x_copy(b).start()
    start_key()

    barrier = pltpu.get_barrier_semaphore()
    for peer in ({"cp": cp ^ 1}, {"cp": cp ^ 2}, {"tp": tp ^ 1}, {"tp": 3 - tp}):
        pl.semaphore_signal(barrier, inc=1, device_id=peer, device_id_type=MESH)

    lane = lax.broadcasted_iota(jnp.int32, (rows, HEAD), 1)
    both = table[...]
    swapped = pltpu.roll(both, HEAD // 2, 1)
    cos_ref[...] = jnp.where(lane < HEAD // 2, both, swapped)
    sin_ref[...] = jnp.where(lane < HEAD // 2, -swapped, both)

    for b in range(PIECES):
        x_copy(b).wait()
        if b == 0:
            start_value()
        elif b <= 2:
            start_query(b - 1)

        def norm_rows(i, carry):
            sl = pl.ds(pl.multiple_of(b * piece_rows + i * 16, 16), 16)
            xf = xbuf[sl, :].astype(jnp.float32)
            inv = lax.rsqrt(jnp.mean(xf * xf, axis=-1, keepdims=True) + EPS)
            hbuf[sl, :] = (xf * inv * gain[...].astype(jnp.float32)).astype(jnp.bfloat16)
            return carry

        lax.fori_loop(0, piece_rows // 16, norm_rows, 0, unroll=2 if piece_rows >= 32 else 1)

    def project(w_ref, first, count, copy_of):
        def piece_step(piece, carry):
            copy_of(piece).wait()
            prod = jnp.dot(hbuf[first:first + count, pl.ds(pl.multiple_of(piece * depth, depth), depth)],
                           w_ref[piece], preferred_element_type=jnp.float32)

            @pl.when(piece == 0)
            def _():
                acc[:count] = prod

            @pl.when(piece > 0)
            def _():
                acc[:count] += prod

            return carry

        lax.fori_loop(0, 4, piece_step, 0)

    def roped(head, first, count):
        vals = acc[:count, head * HEAD:(head + 1) * HEAD]
        sl = slice(first, first + count)
        return (vals * cos_ref[sl] + pltpu.roll(vals, HEAD // 2, 1) * sin_ref[sl]).astype(jnp.bfloat16)

    def kv_copy(slot, part_id, sem, target):
        heads = pl.ds(2 * part_id, 2)
        return pltpu.make_async_remote_copy(src_ref=kvbuf.at[slot, heads], dst_ref=kvbuf.at[slot, heads],
                                            send_sem=kv_send.at[part_id, sem], recv_sem=kv_recv.at[part_id, slot],
                                            device_id={"cp": target}, device_id_type=MESH)

    def send_own(part_id):
        @pl.when(cp == 0)
        def _():
            kv_copy(0, part_id, 0, 2).start()
            kv_copy(0, part_id, 1, 1).start()

        @pl.when(cp == 1)
        def _():
            kv_copy(1, part_id, 0, 3).start()

        @pl.when(cp == 2)
        def _():
            kv_copy(2, part_id, 0, 3).start()

    def relay(part_id):
        @pl.when(cp == 2)
        def _():
            kv_copy(0, part_id, 1, 3).wait_recv()
            kv_copy(0, part_id, 1, 3).start()

        @pl.when(cp == 3)
        def _():
            kv_copy(1, part_id, 1, 2).wait_recv()
            kv_copy(1, part_id, 1, 2).start()

    project(wbuf.at[0], 0, rows, lambda piece: col_tile(w_key, 0, 0, piece))
    start_query(2)
    for head in range(2):
        roped_key = roped(head, 0, rows)
        kvbuf[cp, head] = roped_key
        k_out[head] = roped_key
    pl.semaphore_wait(barrier, 4)
    send_own(0)
    project(wbuf.at[1], 0, rows, lambda piece: col_tile(w_value, 0, 1, piece))
    start_query(3)
    for head in range(2):
        value = acc[:, head * HEAD:(head + 1) * HEAD].astype(jnp.bfloat16)
        kvbuf[cp, 2 + head] = value
        v_out[head] = value
    send_own(1)

    for piece in range(4):
        late_tile(0, piece).start()

    def query_step(j, carry):
        slot = lax.rem(j + 2, RING)
        project(wbuf.at[slot], 0, half,
                lambda piece: col_tile(w_query, pl.multiple_of(j * TILE, TILE), slot, piece))

        @pl.when(j + RING < q_tiles)
        def _():
            start_query(j + RING)

        @pl.when(j + RING >= q_tiles)
        def _():
            start_out(j + RING - q_tiles)

        for head in range(2):
            qbuf[j, head, :half] = roped(head, 0, half)

        @pl.when(j == q_tiles // 2)
        def _():
            relay(0)

        return carry

    lax.fori_loop(0, q_tiles, query_step, 0)
    relay(1)

    for part_id in range(2):
        @pl.when(cp == 1)
        def _():
            kv_copy(0, part_id, 0, 0).wait_recv()

        @pl.when(cp == 2)
        def _():
            kv_copy(1, part_id, 0, 0).wait_recv()

        @pl.when(cp == 3)
        def _():
            kv_copy(2, part_id, 0, 0).wait_recv()
            kv_copy(0, part_id, 0, 0).wait_recv()

    def late_queries(j):
        project(w_late, half, half, lambda piece: late_tile(j, piece))

        @pl.when(j + 1 < q_tiles)
        def _():
            for piece in range(4):
                late_tile(j + 1, piece).start()

        for head in range(2):
            qbuf[j, head, half:] = roped(head, half, half)

    def attend(b, j):
        kv_head = lax.div(4 * j, group)
        qs = qbuf[pl.ds(2 * j, 2), :, pl.ds(pl.multiple_of(b * br, br), br), :].reshape(4 * br, HEAD)

        def scores_of(slot):
            return lax.dot_general(qs, kvbuf[slot, kv_head], (((1,), (1,)), ((), ())),
                                   preferred_element_type=jnp.float32)

        scores = scores_of(cp)
        row = lax.broadcasted_iota(jnp.int32, scores.shape, 0) % br + b * br
        key = lax.broadcasted_iota(jnp.int32, scores.shape, 1)
        scores = jnp.where(key <= row, scores, -jnp.inf)
        top = jnp.max(scores, axis=-1, keepdims=True)
        probs = jnp.exp2((scores - top) * EXP2_SCALE)
        total = jnp.sum(probs, axis=-1, keepdims=True)
        mixed = jnp.dot(probs.astype(jnp.bfloat16), kvbuf[cp, 2 + kv_head], preferred_element_type=jnp.float32)

        def earlier(slot, carry):
            top, total, mixed = carry
            scores = scores_of(slot)
            new_top = jnp.maximum(top, jnp.max(scores, axis=-1, keepdims=True))
            fade = jnp.exp2((top - new_top) * EXP2_SCALE)
            probs = jnp.exp2((scores - new_top) * EXP2_SCALE)
            total = total * fade + jnp.sum(probs, axis=-1, keepdims=True)
            mixed = mixed * fade + jnp.dot(probs.astype(jnp.bfloat16), kvbuf[slot, 2 + kv_head],
                                           preferred_element_type=jnp.float32)
            return new_top, total, mixed

        top, total, mixed = lax.fori_loop(0, cp, earlier, (top, total, mixed))
        attn = (mixed / total).astype(jnp.bfloat16)
        for i in range(2):
            obuf[lax.rem(b, 2), 2 * j + i] = jnp.concatenate(
                [attn[2 * i * br:(2 * i + 1) * br], attn[(2 * i + 1) * br:(2 * i + 2) * br]], axis=1)

    def first_block(j, carry):
        attend(0, j)
        return carry

    lax.fori_loop(0, q_tiles // 2, first_block, 0)

    def chunk(ref, t):
        b, j = lax.div(t, chunks), lax.rem(t, chunks)
        return ref.at[pl.ds(pl.multiple_of(b * br, br), br), pl.ds(pl.multiple_of(j * COLS, COLS), COLS)]

    def partial_copy(t):
        return pltpu.make_async_remote_copy(src_ref=chunk(buf_a, t), dst_ref=chunk(buf_a, t),
                                            send_sem=send_a.at[t], recv_sem=recv_a.at[t],
                                            device_id={"tp": tp ^ 1}, device_id_type=MESH)

    def pair_copy(t):
        return pltpu.make_async_remote_copy(src_ref=chunk(buf_a, t), dst_ref=chunk(buf_b, t),
                                            send_sem=send_a.at[t], recv_sem=recv_b.at[t],
                                            device_id={"tp": 3 - tp}, device_id_type=MESH)

    def final_copy(t):
        return pltpu.make_async_remote_copy(src_ref=chunk(buf_b, t), dst_ref=chunk(buf_b, t),
                                            send_sem=send_b.at[t], recv_sem=recv_b.at[t],
                                            device_id={"tp": tp ^ 1}, device_id_type=MESH)

    def finish(t):
        pair_copy(t).wait_recv()
        mine, theirs, res = chunk(buf_a, t), chunk(buf_b, t), chunk(xbuf, t)
        attn_sum = mine[...].astype(jnp.float32) + theirs[...].astype(jnp.float32)
        theirs[...] = (res[...].astype(jnp.float32) + attn_sum).astype(jnp.bfloat16)
        final_copy(t).start()

    def tick(t, carry):
        b, j = lax.div(t, chunks), lax.rem(t, chunks)
        slot = lax.rem(t + 2 + q_tiles, RING)
        col = pl.multiple_of(j * COLS, COLS)
        for piece in range(4):
            out_tile(col, slot, piece).wait()
        lhs = jnp.concatenate([obuf[lax.rem(b, 2), i] for i in range(q_tiles)], axis=1)
        for piece in range(4):
            part[:, piece * TILE:(piece + 1) * TILE] = jnp.dot(lhs, wbuf[slot, piece],
                                                              preferred_element_type=jnp.float32)

        @pl.when(t + RING < ticks)
        def _():
            start_out(t + RING)

        @pl.when(is_outer)
        def _():
            chunk(buf_a, t)[...] = part[...].astype(jnp.bfloat16)
            partial_copy(t).start()

        @pl.when(jnp.logical_and(is_inner, t >= 2))
        def _():
            finish(t - 2)

        @pl.when(jnp.logical_and(b + 1 < BLOCKS, lax.rem(j, 2) == 0))
        def _():
            attend(b + 1, lax.div(j, 2))

        @pl.when(jnp.logical_and(b < 2, lax.rem(j, 2) == 1))
        def _():
            late_queries(b * (chunks // 2) + lax.div(j, 2))

        @pl.when(is_inner)
        def _():
            partial_copy(t).wait_recv()
            mine = chunk(buf_a, t)
            mine[...] = (part[...] + mine[...].astype(jnp.float32)).astype(jnp.bfloat16)
            pair_copy(t).start()

        return carry

    lax.fori_loop(0, ticks, tick, 0)

    @pl.when(is_inner)
    def _():
        finish(ticks - 2)
        finish(ticks - 1)

        def drain(t, carry):
            pair_copy(t).wait_send()
            final_copy(t).wait_send()
            return carry

        lax.fori_loop(0, ticks, drain, 0)

    @pl.when(is_outer)
    def _():
        def drain(t, carry):
            partial_copy(t).wait_send()
            final_copy(t).wait_recv()
            return carry

        lax.fori_loop(0, ticks, drain, 0)

    for part_id in range(2):
        @pl.when(cp == 0)
        def _():
            kv_copy(0, part_id, 0, 2).wait_send()
            kv_copy(0, part_id, 1, 1).wait_send()

        @pl.when(cp == 1)
        def _():
            kv_copy(1, part_id, 0, 3).wait_send()

        @pl.when(cp == 2)
        def _():
            kv_copy(2, part_id, 0, 3).wait_send()
            kv_copy(0, part_id, 1, 3).wait_send()

        @pl.when(cp == 3)
        def _():
            kv_copy(1, part_id, 1, 2).wait_send()


def solution(mesh):
    row_spec = P(('dp', 'cp'), None)
    cache_spec = P(('dp', 'cp'), 'tp', None)
    head_cols = P(None, 'tp')

    def local_block(hidden, positions, norm_gain, w_query, w_key, w_value, w_out):
        rows, width = hidden.shape
        depth = w_query.shape[1]
        q_tiles = depth // TILE
        kv_cols = w_key.shape[1]
        br = rows // BLOCKS
        ticks = BLOCKS * (width // COLS)
        any_spec = pl.BlockSpec(memory_space=pl.ANY)
        vmem_spec = pl.BlockSpec(memory_space=pltpu.VMEM)
        bf16, f32 = jnp.bfloat16, jnp.float32
        dma = pltpu.SemaphoreType.DMA
        held = 2 * rows * (width + 2 * TILE)
        out, keys, values = pl.pallas_call(
            block_kernel,
            out_shape=(pltpu.VMEM((rows, width), bf16), pltpu.VMEM((2, rows, HEAD), bf16),
                       pltpu.VMEM((2, rows, HEAD), bf16)),
            in_specs=[any_spec, vmem_spec, vmem_spec, any_spec, any_spec, any_spec, any_spec],
            out_specs=(vmem_spec, vmem_spec, vmem_spec),
            scratch_shapes=[
                pltpu.VMEM((rows, width), bf16),
                pltpu.VMEM((rows, width), bf16),
                pltpu.VMEM((RING, 4, depth, TILE), bf16),
                pltpu.VMEM((4, depth, TILE), bf16),
                pltpu.VMEM((q_tiles, 2, rows, HEAD), bf16),
                pltpu.VMEM((4, 4, rows, HEAD), bf16),
                pltpu.VMEM((2, q_tiles, br, TILE), bf16),
                pltpu.VMEM((rows, TILE), f32),
                pltpu.VMEM((br, COLS), f32),
                pltpu.VMEM((rows, width), bf16),
                pltpu.VMEM((rows, HEAD), f32),
                pltpu.VMEM((rows, HEAD), f32),
                dma((PIECES,)), dma((RING, 4)), dma((4,)), dma((2, 2)), dma((2, 4)),
                dma((ticks,)), dma((ticks,)), dma((ticks,)), dma((ticks,)),
            ],
            compiler_params=pltpu.CompilerParams(collective_id=0, has_side_effects=True,
                                                 vmem_limit_bytes=67043328 - held - 65536),
            name="attention_block",
        )(hidden, norm_gain.reshape(1, width), rope_table(positions), w_query, w_key, w_value, w_out)
        return out, jnp.transpose(keys, (1, 0, 2)), jnp.transpose(values, (1, 0, 2))

    return jax.shard_map(local_block, mesh=mesh, in_specs=(row_spec, P(('dp', 'cp')), P(None), head_cols, head_cols, head_cols, P('tp', None)), out_specs=(row_spec, cache_spec, cache_spec), check_vma=False)
```

time: 272 us -> 249 us (0.915)
  Pallas kernels: 257 us -> 239 us
  local copies, waits for them, and re-layouts: 12.1 us -> 6.69 us
    pallas_call x1, Pallas kernels: 257 us -> 239 us  [local_block(): pl.pallas_call(block_kernel, out_shape=(pltpu.VMEM((rows, width), bf16),...]
    unnamed x3, local copies, waits for them, and re-layouts: 9.72 us -> 5.34 us
where the time goes in v2:
time: 249 us
  Pallas kernels  239 us (96%)
  local copies, waits for them, and re-layouts  6.69 us (3%)
    pallas_call x1, Pallas kernels, local_block(): pl.pallas_call(block_kernel, out_shape=(pltpu.VMEM((rows, width), bf16),...  239 us
    unnamed x3, local copies, waits for them, and re-layouts  5.34 us

profile of v2, /device:TPU:7, one launch (start us, length us, event | category | flops | bytes accessed | tf_op | source)
XLA Modules:
  0.0 248.6 jit_solution(8428916761499966393)
XLA Ops:
  0.7 0.7 convert_element_type.10
  1.3 1.3 reshape.22.gain
  2.7 1.8 fusion.table
  4.4 238.8 %attention_block.1 = (bf16[512,8192]{1,0:T(8,128)(2,1)S(1)}, bf16[2,512,128]{2,1,0:T(8,128)(2,1)S(1)}, bf16[2,512,128]{2,1,0:T(8,128)(2,1)S(1)}) custom-call(bf16[512,8192]{1,0:T(8,128)(2,1)} %hidden.1, bf16[1,8192]{1,0:T(2,128)(2,1)} %reshape.22.gain, f32[512,128]{1,0:T(8,128)} %fusion.table, bf16[8192,2048]{1,0:T(8,128)(2,1)} %w_query.1, ...), custom_call_target="tpu_custom_call" | custom-call | tf_op jit(solution)/shard_map/attention_block/pallas_call | solution.py:402
  243.2 3.4 %copy.13 = bf16[512,8192]{1,0:T(8,128)(2,1)} copy(bf16[512,8192]{1,0:T(8,128)(2,1)S(1)} %get-tuple-element.12) | data formatting | bytes 16777216
  246.6 1.0 copy.10
  247.6 1.0 copy.11
  (2 shorter events, 0.0 us)

commit v3 on v2

--- a/solution.py
+++ b/solution.py
@@ -19,18 +19,17 @@
 RING = 4
 
 
-def rope_table(positions):
+def rope_tables(positions):
     half_dim = HEAD // 2
-    lane = jnp.arange(HEAD, dtype=jnp.int32)
-    inv_freq = jnp.exp((lane % half_dim).astype(jnp.float32) * (-2.0 * LOG_THETA / HEAD))
+    inv_freq = jnp.exp(jnp.arange(half_dim, dtype=jnp.float32) * (-2.0 * LOG_THETA / HEAD))
     angles = positions.astype(jnp.float32)[..., None] * inv_freq
-    return jnp.where(lane < half_dim, jnp.cos(angles), jnp.sin(angles))
-
-
-def block_kernel(hidden, gain, table, w_query, w_key, w_value, w_out,
+    return jnp.cos(angles), jnp.sin(angles)
+
+
+def block_kernel(hidden, gain, cos_in, sin_in, w_query, w_key, w_value, w_out,
                  buf_b, k_out, v_out,
                  xbuf, hbuf, wbuf, w_late, qbuf, kvbuf, obuf, acc, part, buf_a, cos_ref, sin_ref,
-                 xsem, wsem, late_sem, kv_send, kv_recv, send_a, recv_a, send_b, recv_b):
+                 gain_raw, gain_row, cos_half, sin_half, inv_ref, small_sem, xsem, wsem, late_sem, kv_send, kv_recv, send_a, recv_a, send_b, recv_b):
     rows, width = xbuf.shape
     q_tiles = qbuf.shape[0]
     depth = wbuf.shape[2]
@@ -79,7 +78,14 @@
         for piece in range(4):
             out_tile(col, lax.rem(t + 2 + q_tiles, RING), piece).start()
 
-    for b in range(PIECES):
+    small = (pltpu.make_async_copy(gain, gain_raw, small_sem.at[0]),
+             pltpu.make_async_copy(cos_in, cos_half, small_sem.at[1]),
+             pltpu.make_async_copy(sin_in, sin_half, small_sem.at[2]))
+    small[0].start()
+    x_copy(0).start()
+    small[1].start()
+    small[2].start()
+    for b in range(1, PIECES):
         x_copy(b).start()
     start_key()
 
@@ -87,11 +93,9 @@
     for peer in ({"cp": cp ^ 1}, {"cp": cp ^ 2}, {"tp": tp ^ 1}, {"tp": 3 - tp}):
         pl.semaphore_signal(barrier, inc=1, device_id=peer, device_id_type=MESH)
 
-    lane = lax.broadcasted_iota(jnp.int32, (rows, HEAD), 1)
-    both = table[...]
-    swapped = pltpu.roll(both, HEAD // 2, 1)
-    cos_ref[...] = jnp.where(lane < HEAD // 2, both, swapped)
-    sin_ref[...] = jnp.where(lane < HEAD // 2, -swapped, both)
+    small[0].wait()
+    for c in range(width // HEAD):
+        gain_row[:, c * HEAD:(c + 1) * HEAD] = gain_raw[c:c + 1, :].astype(jnp.float32)
 
     for b in range(PIECES):
         x_copy(b).wait()
@@ -100,14 +104,32 @@
         elif b <= 2:
             start_query(b - 1)
 
+        def square_rows(i, carry):
+            sl = pl.ds(pl.multiple_of(b * piece_rows + i * 16, 16), 16)
+            sums = [jnp.zeros((16, HEAD), jnp.float32) for _ in range(4)]
+            for c in range(width // HEAD):
+                xf = xbuf[sl, c * HEAD:(c + 1) * HEAD].astype(jnp.float32)
+                sums[c % 4] += xf * xf
+            mean = jnp.sum((sums[0] + sums[1]) + (sums[2] + sums[3]), axis=-1, keepdims=True) / width
+            inv_ref[sl, :] = jnp.broadcast_to(lax.rsqrt(mean + EPS), (16, HEAD))
+            return carry
+
+        lax.fori_loop(0, piece_rows // 16, square_rows, 0, unroll=2 if piece_rows >= 32 else 1)
+
         def norm_rows(i, carry):
             sl = pl.ds(pl.multiple_of(b * piece_rows + i * 16, 16), 16)
-            xf = xbuf[sl, :].astype(jnp.float32)
-            inv = lax.rsqrt(jnp.mean(xf * xf, axis=-1, keepdims=True) + EPS)
-            hbuf[sl, :] = (xf * inv * gain[...].astype(jnp.float32)).astype(jnp.bfloat16)
+            inv = inv_ref[sl, :]
+            for c in range(width // HEAD):
+                cols = slice(c * HEAD, (c + 1) * HEAD)
+                hbuf[sl, cols] = (xbuf[sl, cols].astype(jnp.float32) * inv * gain_row[:, cols]).astype(jnp.bfloat16)
             return carry
 
-        lax.fori_loop(0, piece_rows // 16, norm_rows, 0, unroll=2 if piece_rows >= 32 else 1)
+        lax.fori_loop(0, piece_rows // 16, norm_rows, 0)
+
+    small[1].wait()
+    small[2].wait()
+    cos_ref[...] = jnp.concatenate([cos_half[...], cos_half[...]], axis=1)
+    sin_ref[...] = jnp.concatenate([-sin_half[...], sin_half[...]], axis=1)
 
     def project(w_ref, first, count, copy_of):
         def piece_step(piece, carry):
@@ -318,10 +340,6 @@
             chunk(buf_a, t)[...] = part[...].astype(jnp.bfloat16)
             partial_copy(t).start()
 
-        @pl.when(jnp.logical_and(is_inner, t >= 2))
-        def _():
-            finish(t - 2)
-
         @pl.when(jnp.logical_and(b + 1 < BLOCKS, lax.rem(j, 2) == 0))
         def _():
             attend(b + 1, lax.div(j, 2))
@@ -336,6 +354,10 @@
             mine = chunk(buf_a, t)
             mine[...] = (part[...] + mine[...].astype(jnp.float32)).astype(jnp.bfloat16)
             pair_copy(t).start()
+
+        @pl.when(jnp.logical_and(is_inner, t >= 2))
+        def _():
+            finish(t - 2)
 
         return carry
 
@@ -403,7 +425,7 @@
             block_kernel,
             out_shape=(pltpu.VMEM((rows, width), bf16), pltpu.VMEM((2, rows, HEAD), bf16),
                        pltpu.VMEM((2, rows, HEAD), bf16)),
-            in_specs=[any_spec, vmem_spec, vmem_spec, any_spec, any_spec, any_spec, any_spec],
+            in_specs=[any_spec] * 8,
             out_specs=(vmem_spec, vmem_spec, vmem_spec),
             scratch_shapes=[
                 pltpu.VMEM((rows, width), bf16),
@@ -418,13 +440,18 @@
                 pltpu.VMEM((rows, width), bf16),
                 pltpu.VMEM((rows, HEAD), f32),
                 pltpu.VMEM((rows, HEAD), f32),
-                dma((PIECES,)), dma((RING, 4)), dma((4,)), dma((2, 2)), dma((2, 4)),
+                pltpu.VMEM((width // HEAD, HEAD), bf16),
+                pltpu.VMEM((1, width), f32),
+                pltpu.VMEM((rows, HEAD // 2), f32),
+                pltpu.VMEM((rows, HEAD // 2), f32),
+                pltpu.VMEM((rows, HEAD), f32),
+                dma((3,)), dma((PIECES,)), dma((RING, 4)), dma((4,)), dma((2, 2)), dma((2, 4)),
                 dma((ticks,)), dma((ticks,)), dma((ticks,)), dma((ticks,)),
             ],
             compiler_params=pltpu.CompilerParams(collective_id=0, has_side_effects=True,
                                                  vmem_limit_bytes=67043328 - held - 65536),
             name="attention_block",
-        )(hidden, norm_gain.reshape(1, width), rope_table(positions), w_query, w_key, w_value, w_out)
+        )(hidden, norm_gain.reshape(width // HEAD, HEAD), *rope_tables(positions), w_query, w_key, w_value, w_out)
         return out, jnp.transpose(keys, (1, 0, 2)), jnp.transpose(values, (1, 0, 2))
 
     return jax.shard_map(local_block, mesh=mesh, in_specs=(row_spec, P(('dp', 'cp')), P(None), head_cols, head_cols, head_cols, P('tp', None)), out_specs=(row_spec, cache_spec, cache_spec), check_vma=False)

time: 249 us -> 244 us (0.980)
  Pallas kernels: 239 us -> 235 us
    pallas_call x1, Pallas kernels: 239 us -> 235 us  [local_block(): pl.pallas_call(block_kernel, out_shape=(pltpu.VMEM((rows, width), bf16),...]
where the time goes in v3:
time: 244 us; the launch traced here: 243 us
  Pallas kernels  235 us (96%)
  local copies, waits for them, and re-layouts  5.34 us (2%)
  other arithmetic  2.49 us (1%)
    pallas_call x1, Pallas kernels, local_block(): pl.pallas_call(block_kernel, out_shape=(pltpu.VMEM((rows, width), bf16),...  235 us
    unnamed x3, local copies, waits for them, and re-layouts  5.34 us

profile of v3, /device:TPU:7, one launch (start us, length us, event | category | flops | bytes accessed | tf_op | source)
XLA Modules:
  0.0 243.5 jit_solution(6474134210761553818)
XLA Ops:
  0.6 0.7 convert_element_type.3
  1.3 1.8 multiply_sine_fusion
  3.1 235.0 %attention_block.1 = (bf16[512,8192]{1,0:T(8,128)(2,1)S(1)}, bf16[2,512,128]{2,1,0:T(8,128)(2,1)S(1)}, bf16[2,512,128]{2,1,0:T(8,128)(2,1)S(1)}) custom-call(bf16[512,8192]{1,0:T(8,128)(2,1)} %hidden.1, bf16[64,128]{1,0:T(8,128)(2,1)} %bitcast.5, f32[512,64]{1,0:T(8,128)} %get-tuple-element.13.cos_in, f32[512,64]{1,0:T(8,128)} %get-tuple-element.12.sin_in, ...), custom_call_target="tpu_custom_call" | custom-call | tf_op jit(solution)/shard_map/attention_block/pallas_call | solution.py:424
  238.1 3.4 %copy.13 = bf16[512,8192]{1,0:T(8,128)(2,1)} copy(bf16[512,8192]{1,0:T(8,128)(2,1)S(1)} %get-tuple-element.14) | data formatting | bytes 16777216
  241.5 1.0 copy.10
  242.5 1.0 copy.11
  (1 shorter events, 0.0 us)

commit v4 on v3

--- a/solution.py
+++ b/solution.py
@@ -13,7 +13,9 @@
 EXP2_SCALE = math.log2(math.e) / math.sqrt(HEAD)
 MESH = pl.DeviceIdType.MESH
 BLOCKS = 8
-PIECES = 4
+PIECES = 8
+SUBS = 2
+LAG = 3
 COLS = 1024
 TILE = 256
 RING = 4
@@ -32,7 +34,7 @@
                  gain_raw, gain_row, cos_half, sin_half, inv_ref, small_sem, xsem, wsem, late_sem, kv_send, kv_recv, send_a, recv_a, send_b, recv_b):
     rows, width = xbuf.shape
     q_tiles = qbuf.shape[0]
-    depth = wbuf.shape[2]
+    depth = wbuf.shape[1] // 4
     br = rows // BLOCKS
     piece_rows = rows // PIECES
     half = rows // 2
@@ -50,16 +52,16 @@
 
     def col_tile(w_ref, col, slot, piece):
         return pltpu.make_async_copy(w_ref.at[pl.ds(piece * depth, depth), pl.ds(col, TILE)],
-                                     wbuf.at[slot, piece], wsem.at[slot, piece])
+                                     wbuf.at[slot, pl.ds(piece * depth, depth)], wsem.at[slot, piece])
 
     def late_tile(j, piece):
         return pltpu.make_async_copy(
             w_query.at[pl.ds(piece * depth, depth), pl.ds(pl.multiple_of(j * TILE, TILE), TILE)],
-            w_late.at[piece], late_sem.at[piece])
+            w_late.at[pl.ds(piece * depth, depth)], late_sem.at[piece])
 
     def out_tile(col, slot, piece):
         return pltpu.make_async_copy(w_out.at[:, pl.ds(col + piece * TILE, TILE)],
-                                     wbuf.at[slot, piece], wsem.at[slot, piece])
+                                     wbuf.at[slot, pl.ds(piece * depth, depth)], wsem.at[slot, piece])
 
     def start_key():
         for piece in range(4):
@@ -82,12 +84,8 @@
              pltpu.make_async_copy(cos_in, cos_half, small_sem.at[1]),
              pltpu.make_async_copy(sin_in, sin_half, small_sem.at[2]))
     small[0].start()
-    x_copy(0).start()
-    small[1].start()
-    small[2].start()
-    for b in range(1, PIECES):
+    for b in range(3):
         x_copy(b).start()
-    start_key()
 
     barrier = pltpu.get_barrier_semaphore()
     for peer in ({"cp": cp ^ 1}, {"cp": cp ^ 2}, {"tp": tp ^ 1}, {"tp": 3 - tp}):
@@ -97,13 +95,7 @@
     for c in range(width // HEAD):
         gain_row[:, c * HEAD:(c + 1) * HEAD] = gain_raw[c:c + 1, :].astype(jnp.float32)
 
-    for b in range(PIECES):
-        x_copy(b).wait()
-        if b == 0:
-            start_value()
-        elif b <= 2:
-            start_query(b - 1)
-
+    def normalize(b):
         def square_rows(i, carry):
             sl = pl.ds(pl.multiple_of(b * piece_rows + i * 16, 16), 16)
             sums = [jnp.zeros((16, HEAD), jnp.float32) for _ in range(4)]
@@ -126,37 +118,17 @@
 
         lax.fori_loop(0, piece_rows // 16, norm_rows, 0)
 
-    small[1].wait()
-    small[2].wait()
-    cos_ref[...] = jnp.concatenate([cos_half[...], cos_half[...]], axis=1)
-    sin_ref[...] = jnp.concatenate([-sin_half[...], sin_half[...]], axis=1)
-
-    def project(w_ref, first, count, copy_of):
-        def piece_step(piece, carry):
-            copy_of(piece).wait()
-            prod = jnp.dot(hbuf[first:first + count, pl.ds(pl.multiple_of(piece * depth, depth), depth)],
-                           w_ref[piece], preferred_element_type=jnp.float32)
-
-            @pl.when(piece == 0)
-            def _():
-                acc[:count] = prod
-
-            @pl.when(piece > 0)
-            def _():
-                acc[:count] += prod
-
-            return carry
-
-        lax.fori_loop(0, 4, piece_step, 0)
-
-    def roped(head, first, count):
-        vals = acc[:count, head * HEAD:(head + 1) * HEAD]
-        sl = slice(first, first + count)
+    def project(w_ref, first):
+        acc[...] = jnp.dot(hbuf[pl.ds(first, half), :], w_ref[...], preferred_element_type=jnp.float32)
+
+    def roped(head, first):
+        vals = acc[:, head * HEAD:(head + 1) * HEAD]
+        sl = pl.ds(first, half)
         return (vals * cos_ref[sl] + pltpu.roll(vals, HEAD // 2, 1) * sin_ref[sl]).astype(jnp.bfloat16)
 
     def kv_copy(slot, part_id, sem, target):
-        heads = pl.ds(2 * part_id, 2)
-        return pltpu.make_async_remote_copy(src_ref=kvbuf.at[slot, heads], dst_ref=kvbuf.at[slot, heads],
+        where = (slot, pl.ds(2 * (part_id % 2), 2), pl.ds(part_id // 2 * half, half))
+        return pltpu.make_async_remote_copy(src_ref=kvbuf.at[where], dst_ref=kvbuf.at[where],
                                             send_sem=kv_send.at[part_id, sem], recv_sem=kv_recv.at[part_id, slot],
                                             device_id={"cp": target}, device_id_type=MESH)
 
@@ -185,29 +157,57 @@
             kv_copy(1, part_id, 1, 2).wait_recv()
             kv_copy(1, part_id, 1, 2).start()
 
-    project(wbuf.at[0], 0, rows, lambda piece: col_tile(w_key, 0, 0, piece))
-    start_query(2)
-    for head in range(2):
-        roped_key = roped(head, 0, rows)
-        kvbuf[cp, head] = roped_key
-        k_out[head] = roped_key
-    pl.semaphore_wait(barrier, 4)
-    send_own(0)
-    project(wbuf.at[1], 0, rows, lambda piece: col_tile(w_value, 0, 1, piece))
-    start_query(3)
-    for head in range(2):
-        value = acc[:, head * HEAD:(head + 1) * HEAD].astype(jnp.bfloat16)
-        kvbuf[cp, 2 + head] = value
-        v_out[head] = value
-    send_own(1)
+    for hf in range(2):
+        first = hf * half
+        for b in range(hf * PIECES // 2, (hf + 1) * PIECES // 2):
+            x_copy(b).wait()
+            if b + 3 < PIECES:
+                x_copy(b + 3).start()
+            if b == 0:
+                start_key()
+            elif b == 1:
+                start_value()
+                small[1].start()
+                small[2].start()
+            elif b in (PIECES // 2, PIECES // 2 + 1):
+                start_query(b - PIECES // 2)
+            normalize(b)
+        if hf == 0:
+            small[1].wait()
+            small[2].wait()
+            cos_ref[...] = jnp.concatenate([cos_half[...], cos_half[...]], axis=1)
+            sin_ref[...] = jnp.concatenate([-sin_half[...], sin_half[...]], axis=1)
+            for piece in range(4):
+                col_tile(w_key, 0, 0, piece).wait()
+        project(wbuf.at[0], first)
+        if hf == 1:
+            start_query(2)
+        for head in range(2):
+            key = roped(head, first)
+            kvbuf[cp, head, first:first + half] = key
+            k_out[head, first:first + half] = key
+        if hf == 0:
+            pl.semaphore_wait(barrier, 4)
+            for piece in range(4):
+                col_tile(w_value, 0, 1, piece).wait()
+        send_own(2 * hf)
+        project(wbuf.at[1], first)
+        if hf == 1:
+            start_query(3)
+        for head in range(2):
+            value = acc[:, head * HEAD:(head + 1) * HEAD].astype(jnp.bfloat16)
+            kvbuf[cp, 2 + head, first:first + half] = value
+            v_out[head, first:first + half] = value
+        send_own(2 * hf + 1)
 
     for piece in range(4):
         late_tile(0, piece).start()
 
     def query_step(j, carry):
         slot = lax.rem(j + 2, RING)
-        project(wbuf.at[slot], 0, half,
-                lambda piece: col_tile(w_query, pl.multiple_of(j * TILE, TILE), slot, piece))
+        for piece in range(4):
+            col_tile(w_query, pl.multiple_of(j * TILE, TILE), slot, piece).wait()
+        project(wbuf.at[slot], 0)
 
         @pl.when(j + RING < q_tiles)
         def _():
@@ -218,18 +218,18 @@
             start_out(j + RING - q_tiles)
 
         for head in range(2):
-            qbuf[j, head, :half] = roped(head, 0, half)
-
-        @pl.when(j == q_tiles // 2)
-        def _():
-            relay(0)
+            qbuf[j, head, :half] = roped(head, 0)
+
+        for part_id in range(4):
+            @pl.when(j == part_id * q_tiles // 4)
+            def _():
+                relay(part_id)
 
         return carry
 
     lax.fori_loop(0, q_tiles, query_step, 0)
-    relay(1)
-
-    for part_id in range(2):
+
+    for part_id in range(4):
         @pl.when(cp == 1)
         def _():
             kv_copy(0, part_id, 0, 0).wait_recv()
@@ -244,7 +244,9 @@
             kv_copy(0, part_id, 0, 0).wait_recv()
 
     def late_queries(j):
-        project(w_late, half, half, lambda piece: late_tile(j, piece))
+        for piece in range(4):
+            late_tile(j, piece).wait()
+        project(w_late, half)
 
         @pl.when(j + 1 < q_tiles)
         def _():
@@ -252,7 +254,7 @@
                 late_tile(j + 1, piece).start()
 
         for head in range(2):
-            qbuf[j, head, half:] = roped(head, half, half)
+            qbuf[j, head, half:] = roped(head, half)
 
     def attend(b, j):
         kv_head = lax.div(4 * j, group)
@@ -294,9 +296,13 @@
 
     lax.fori_loop(0, q_tiles // 2, first_block, 0)
 
-    def chunk(ref, t):
-        b, j = lax.div(t, chunks), lax.rem(t, chunks)
-        return ref.at[pl.ds(pl.multiple_of(b * br, br), br), pl.ds(pl.multiple_of(j * COLS, COLS), COLS)]
+    sub_cols = COLS // SUBS
+    copies = ticks * SUBS
+
+    def chunk(ref, u):
+        b, j = lax.div(u, chunks * SUBS), lax.rem(u, chunks * SUBS)
+        return ref.at[pl.ds(pl.multiple_of(b * br, br), br),
+                      pl.ds(pl.multiple_of(j * sub_cols, sub_cols), sub_cols)]
 
     def partial_copy(t):
         return pltpu.make_async_remote_copy(src_ref=chunk(buf_a, t), dst_ref=chunk(buf_a, t),
@@ -328,7 +334,7 @@
             out_tile(col, slot, piece).wait()
         lhs = jnp.concatenate([obuf[lax.rem(b, 2), i] for i in range(q_tiles)], axis=1)
         for piece in range(4):
-            part[:, piece * TILE:(piece + 1) * TILE] = jnp.dot(lhs, wbuf[slot, piece],
+            part[:, piece * TILE:(piece + 1) * TILE] = jnp.dot(lhs, wbuf[slot, piece * depth:(piece + 1) * depth],
                                                               preferred_element_type=jnp.float32)
 
         @pl.when(t + RING < ticks)
@@ -337,8 +343,26 @@
 
         @pl.when(is_outer)
         def _():
-            chunk(buf_a, t)[...] = part[...].astype(jnp.bfloat16)
-            partial_copy(t).start()
+            for i in range(SUBS):
+                chunk(buf_a, t * SUBS + i)[...] = part[:, i * sub_cols:(i + 1) * sub_cols].astype(jnp.bfloat16)
+                partial_copy(t * SUBS + i).start()
+
+        def serve(i):
+            u = t * SUBS + i
+
+            @pl.when(is_inner)
+            def _():
+                partial_copy(u).wait_recv()
+                mine = chunk(buf_a, u)
+                mine[...] = (part[:, i * sub_cols:(i + 1) * sub_cols]
+                             + mine[...].astype(jnp.float32)).astype(jnp.bfloat16)
+                pair_copy(u).start()
+
+            @pl.when(jnp.logical_and(is_inner, u >= LAG))
+            def _():
+                finish(u - LAG)
+
+        serve(0)
 
         @pl.when(jnp.logical_and(b + 1 < BLOCKS, lax.rem(j, 2) == 0))
         def _():
@@ -348,32 +372,23 @@
         def _():
             late_queries(b * (chunks // 2) + lax.div(j, 2))
 
-        @pl.when(is_inner)
-        def _():
-            partial_copy(t).wait_recv()
-            mine = chunk(buf_a, t)
-            mine[...] = (part[...] + mine[...].astype(jnp.float32)).astype(jnp.bfloat16)
-            pair_copy(t).start()
-
-        @pl.when(jnp.logical_and(is_inner, t >= 2))
-        def _():
-            finish(t - 2)
-
+        for i in range(1, SUBS):
+            serve(i)
         return carry
 
     lax.fori_loop(0, ticks, tick, 0)
 
     @pl.when(is_inner)
     def _():
-        finish(ticks - 2)
-        finish(ticks - 1)
+        for u in range(copies - LAG, copies):
+            finish(u)
 
         def drain(t, carry):
             pair_copy(t).wait_send()
             final_copy(t).wait_send()
             return carry
 
-        lax.fori_loop(0, ticks, drain, 0)
+        lax.fori_loop(0, copies, drain, 0)
 
     @pl.when(is_outer)
     def _():
@@ -382,9 +397,9 @@
             final_copy(t).wait_recv()
             return carry
 
-        lax.fori_loop(0, ticks, drain, 0)
-
-    for part_id in range(2):
+        lax.fori_loop(0, copies, drain, 0)
+
+    for part_id in range(4):
         @pl.when(cp == 0)
         def _():
             kv_copy(0, part_id, 0, 2).wait_send()
@@ -415,7 +430,7 @@
         q_tiles = depth // TILE
         kv_cols = w_key.shape[1]
         br = rows // BLOCKS
-        ticks = BLOCKS * (width // COLS)
+        copies = SUBS * BLOCKS * (width // COLS)
         any_spec = pl.BlockSpec(memory_space=pl.ANY)
         vmem_spec = pl.BlockSpec(memory_space=pltpu.VMEM)
         bf16, f32 = jnp.bfloat16, jnp.float32
@@ -430,12 +445,12 @@
             scratch_shapes=[
                 pltpu.VMEM((rows, width), bf16),
                 pltpu.VMEM((rows, width), bf16),
-                pltpu.VMEM((RING, 4, depth, TILE), bf16),
-                pltpu.VMEM((4, depth, TILE), bf16),
+                pltpu.VMEM((RING, width, TILE), bf16),
+                pltpu.VMEM((width, TILE), bf16),
                 pltpu.VMEM((q_tiles, 2, rows, HEAD), bf16),
                 pltpu.VMEM((4, 4, rows, HEAD), bf16),
                 pltpu.VMEM((2, q_tiles, br, TILE), bf16),
-                pltpu.VMEM((rows, TILE), f32),
+                pltpu.VMEM((rows // 2, TILE), f32),
                 pltpu.VMEM((br, COLS), f32),
                 pltpu.VMEM((rows, width), bf16),
                 pltpu.VMEM((rows, HEAD), f32),
@@ -445,8 +460,8 @@
                 pltpu.VMEM((rows, HEAD // 2), f32),
                 pltpu.VMEM((rows, HEAD // 2), f32),
                 pltpu.VMEM((rows, HEAD), f32),
-                dma((3,)), dma((PIECES,)), dma((RING, 4)), dma((4,)), dma((2, 2)), dma((2, 4)),
-                dma((ticks,)), dma((ticks,)), dma((ticks,)), dma((ticks,)),
+                dma((3,)), dma((PIECES,)), dma((RING, 4)), dma((4,)), dma((4, 2)), dma((4, 4)),
+                dma((copies,)), dma((copies,)), dma((copies,)), dma((copies,)),
             ],
             compiler_params=pltpu.CompilerParams(collective_id=0, has_side_effects=True,
                                                  vmem_limit_bytes=67043328 - held - 65536),

time: 244 us -> 241 us (0.988)
  no operation moved by 1% of the time
where the time goes in v4:
time: 241 us
  Pallas kernels  233 us (97%)
  local copies, waits for them, and re-layouts  5.34 us (2%)
  other arithmetic  2.49 us (1%)
    pallas_call x1, Pallas kernels, local_block(): pl.pallas_call(block_kernel, out_shape=(pltpu.VMEM((rows, width), bf16),...  233 us
    unnamed x3, local copies, waits for them, and re-layouts  5.34 us

profile of v4, /device:TPU:7, one launch (start us, length us, event | category | flops | bytes accessed | tf_op | source)
XLA Modules:
  0.0 241.2 jit_solution(5860581793518192074)
XLA Ops:
  0.6 0.7 convert_element_type.3
  1.3 1.8 multiply_sine_fusion
  3.1 232.8 %attention_block.1 = (bf16[512,8192]{1,0:T(8,128)(2,1)S(1)}, bf16[2,512,128]{2,1,0:T(8,128)(2,1)S(1)}, bf16[2,512,128]{2,1,0:T(8,128)(2,1)S(1)}) custom-call(bf16[512,8192]{1,0:T(8,128)(2,1)} %hidden.1, bf16[64,128]{1,0:T(8,128)(2,1)} %bitcast.5, f32[512,64]{1,0:T(8,128)} %get-tuple-element.13.cos_in, f32[512,64]{1,0:T(8,128)} %get-tuple-element.12.sin_in, ...), custom_call_target="tpu_custom_call" | custom-call | tf_op jit(solution)/shard_map/attention_block/pallas_call | solution.py:439
  235.9 3.4 %copy.13 = bf16[512,8192]{1,0:T(8,128)(2,1)} copy(bf16[512,8192]{1,0:T(8,128)(2,1)S(1)} %get-tuple-element.14) | data formatting | bytes 16777216
  239.3 1.0 copy.10
  240.3 1.0 copy.11
  (1 shorter events, 0.0 us)

commit v5 on v4

--- a/solution.py
+++ b/solution.py
@@ -14,8 +14,6 @@
 MESH = pl.DeviceIdType.MESH
 BLOCKS = 8
 PIECES = 8
-SUBS = 2
-LAG = 3
 COLS = 1024
 TILE = 256
 RING = 4
@@ -31,7 +29,7 @@
 def block_kernel(hidden, gain, cos_in, sin_in, w_query, w_key, w_value, w_out,
                  buf_b, k_out, v_out,
                  xbuf, hbuf, wbuf, w_late, qbuf, kvbuf, obuf, acc, part, buf_a, cos_ref, sin_ref,
-                 gain_raw, gain_row, cos_half, sin_half, inv_ref, small_sem, xsem, wsem, late_sem, kv_send, kv_recv, send_a, recv_a, send_b, recv_b):
+                 gain_raw, gain_row, inv_ref, small_sem, xsem, wsem, late_sem, kv_send, kv_recv, send_a, recv_a, send_b, recv_b):
     rows, width = xbuf.shape
     q_tiles = qbuf.shape[0]
     depth = wbuf.shape[1] // 4
@@ -80,10 +78,8 @@
         for piece in range(4):
             out_tile(col, lax.rem(t + 2 + q_tiles, RING), piece).start()
 
-    small = (pltpu.make_async_copy(gain, gain_raw, small_sem.at[0]),
-             pltpu.make_async_copy(cos_in, cos_half, small_sem.at[1]),
-             pltpu.make_async_copy(sin_in, sin_half, small_sem.at[2]))
-    small[0].start()
+    gain_copy = pltpu.make_async_copy(gain, gain_raw, small_sem)
+    gain_copy.start()
     for b in range(3):
         x_copy(b).start()
 
@@ -91,7 +87,7 @@
     for peer in ({"cp": cp ^ 1}, {"cp": cp ^ 2}, {"tp": tp ^ 1}, {"tp": 3 - tp}):
         pl.semaphore_signal(barrier, inc=1, device_id=peer, device_id_type=MESH)
 
-    small[0].wait()
+    gain_copy.wait()
     for c in range(width // HEAD):
         gain_row[:, c * HEAD:(c + 1) * HEAD] = gain_raw[c:c + 1, :].astype(jnp.float32)
 
@@ -167,16 +163,12 @@
                 start_key()
             elif b == 1:
                 start_value()
-                small[1].start()
-                small[2].start()
             elif b in (PIECES // 2, PIECES // 2 + 1):
                 start_query(b - PIECES // 2)
             normalize(b)
         if hf == 0:
-            small[1].wait()
-            small[2].wait()
-            cos_ref[...] = jnp.concatenate([cos_half[...], cos_half[...]], axis=1)
-            sin_ref[...] = jnp.concatenate([-sin_half[...], sin_half[...]], axis=1)
+            cos_ref[...] = jnp.concatenate([cos_in[...], cos_in[...]], axis=1)
+            sin_ref[...] = jnp.concatenate([-sin_in[...], sin_in[...]], axis=1)
             for piece in range(4):
                 col_tile(w_key, 0, 0, piece).wait()
         project(wbuf.at[0], first)
@@ -296,108 +288,143 @@
 
     lax.fori_loop(0, q_tiles // 2, first_block, 0)
 
-    sub_cols = COLS // SUBS
-    copies = ticks * SUBS
-
-    def chunk(ref, u):
-        b, j = lax.div(u, chunks * SUBS), lax.rem(u, chunks * SUBS)
-        return ref.at[pl.ds(pl.multiple_of(b * br, br), br),
-                      pl.ds(pl.multiple_of(j * sub_cols, sub_cols), sub_cols)]
-
-    def partial_copy(t):
-        return pltpu.make_async_remote_copy(src_ref=chunk(buf_a, t), dst_ref=chunk(buf_a, t),
-                                            send_sem=send_a.at[t], recv_sem=recv_a.at[t],
-                                            device_id={"tp": tp ^ 1}, device_id_type=MESH)
-
-    def pair_copy(t):
-        return pltpu.make_async_remote_copy(src_ref=chunk(buf_a, t), dst_ref=chunk(buf_b, t),
-                                            send_sem=send_a.at[t], recv_sem=recv_b.at[t],
-                                            device_id={"tp": 3 - tp}, device_id_type=MESH)
-
-    def final_copy(t):
-        return pltpu.make_async_remote_copy(src_ref=chunk(buf_b, t), dst_ref=chunk(buf_b, t),
-                                            send_sem=send_b.at[t], recv_sem=recv_b.at[t],
-                                            device_id={"tp": tp ^ 1}, device_id_type=MESH)
-
-    def finish(t):
-        pair_copy(t).wait_recv()
-        mine, theirs, res = chunk(buf_a, t), chunk(buf_b, t), chunk(xbuf, t)
-        attn_sum = mine[...].astype(jnp.float32) + theirs[...].astype(jnp.float32)
-        theirs[...] = (res[...].astype(jnp.float32) + attn_sum).astype(jnp.bfloat16)
-        final_copy(t).start()
-
-    def tick(t, carry):
-        b, j = lax.div(t, chunks), lax.rem(t, chunks)
-        slot = lax.rem(t + 2 + q_tiles, RING)
-        col = pl.multiple_of(j * COLS, COLS)
-        for piece in range(4):
-            out_tile(col, slot, piece).wait()
-        lhs = jnp.concatenate([obuf[lax.rem(b, 2), i] for i in range(q_tiles)], axis=1)
-        for piece in range(4):
-            part[:, piece * TILE:(piece + 1) * TILE] = jnp.dot(lhs, wbuf[slot, piece * depth:(piece + 1) * depth],
-                                                              preferred_element_type=jnp.float32)
-
-        @pl.when(t + RING < ticks)
-        def _():
-            start_out(t + RING)
-
-        @pl.when(is_outer)
-        def _():
-            for i in range(SUBS):
-                chunk(buf_a, t * SUBS + i)[...] = part[:, i * sub_cols:(i + 1) * sub_cols].astype(jnp.bfloat16)
-                partial_copy(t * SUBS + i).start()
-
-        def serve(i):
-            u = t * SUBS + i
+    units = ticks // 2
+    wide = 2 * COLS
+    per_row = width // wide
+    LAST = 4
+
+    def chunk(ref, w, i, count):
+        cols = wide // count
+        return ref.at[pl.ds(pl.multiple_of(lax.div(w, per_row) * br, br), br),
+                      pl.ds(pl.multiple_of(lax.rem(w, per_row) * wide + i * cols, cols), cols)]
+
+    def number(w, i, count):
+        return i if count == 2 else (w + 1 if count == 1 else units + 1 + i)
+
+    def copy_of(src, dst, w, i, count, send_sem, recv_sem, target):
+        n = number(w, i, count)
+        return pltpu.make_async_remote_copy(src_ref=chunk(src, w, i, count), dst_ref=chunk(dst, w, i, count),
+                                            send_sem=send_sem.at[n], recv_sem=recv_sem.at[n],
+                                            device_id={"tp": target}, device_id_type=MESH)
+
+    def partial_copy(*where):
+        return copy_of(buf_a, buf_a, *where, send_a, recv_a, tp ^ 1)
+
+    def pair_copy(*where):
+        return copy_of(buf_a, buf_b, *where, send_a, recv_b, 3 - tp)
+
+    def final_copy(*where):
+        return copy_of(buf_b, buf_b, *where, send_b, recv_b, tp ^ 1)
+
+    def send_partial(w, i, count):
+        cols = wide // count
+        chunk(buf_a, w, i, count)[...] = part[:, i * cols:(i + 1) * cols].astype(jnp.bfloat16)
+        partial_copy(w, i, count).start()
+
+    def serve(w, i, count):
+        cols = wide // count
+        partial_copy(w, i, count).wait_recv()
+        mine = chunk(buf_a, w, i, count)
+        mine[...] = (part[:, i * cols:(i + 1) * cols] + mine[...].astype(jnp.float32)).astype(jnp.bfloat16)
+        pair_copy(w, i, count).start()
+
+    def finish(w, count):
+        for i in range(count):
+            pair_copy(w, i, count).wait_recv()
+            mine, theirs, res = chunk(buf_a, w, i, count), chunk(buf_b, w, i, count), chunk(xbuf, w, i, count)
+            attn_sum = mine[...].astype(jnp.float32) + theirs[...].astype(jnp.float32)
+            theirs[...] = (res[...].astype(jnp.float32) + attn_sum).astype(jnp.bfloat16)
+            final_copy(w, i, count).start()
+
+    def unit(w, count, first, last):
+        b = lax.div(w, per_row)
+        pair_id = lax.rem(w, per_row)
+        for odd in range(2):
+            t = 2 * w + odd
+            slot = lax.rem(t + 2 + q_tiles, RING)
+            col = pl.multiple_of((2 * pair_id + odd) * COLS, COLS)
+            for piece in range(4):
+                out_tile(col, slot, piece).wait()
+            lhs = jnp.concatenate([obuf[lax.rem(b, 2), i] for i in range(q_tiles)], axis=1)
+            for piece in range(4):
+                start = odd * COLS + piece * TILE
+                part[:, start:start + TILE] = jnp.dot(lhs, wbuf[slot, piece * depth:(piece + 1) * depth],
+                                                      preferred_element_type=jnp.float32)
+
+            @pl.when(t + RING < ticks)
+            def _():
+                start_out(t + RING)
+
+            mine = range(odd * count // 2, count // 2 + odd * (count - count // 2)) if count > 1 else range(odd)
+
+            @pl.when(is_outer)
+            def _():
+                for i in mine:
+                    send_partial(w, i, count)
+
+            if not last:
+                if odd == 0:
+                    @pl.when(b + 1 < BLOCKS)
+                    def _():
+                        attend(b + 1, pair_id)
+                else:
+                    @pl.when(b < 2)
+                    def _():
+                        late_queries(b * per_row + pair_id)
 
             @pl.when(is_inner)
             def _():
-                partial_copy(u).wait_recv()
-                mine = chunk(buf_a, u)
-                mine[...] = (part[:, i * sub_cols:(i + 1) * sub_cols]
-                             + mine[...].astype(jnp.float32)).astype(jnp.bfloat16)
-                pair_copy(u).start()
-
-            @pl.when(jnp.logical_and(is_inner, u >= LAG))
-            def _():
-                finish(u - LAG)
-
-        serve(0)
-
-        @pl.when(jnp.logical_and(b + 1 < BLOCKS, lax.rem(j, 2) == 0))
-        def _():
-            attend(b + 1, lax.div(j, 2))
-
-        @pl.when(jnp.logical_and(b < 2, lax.rem(j, 2) == 1))
-        def _():
-            late_queries(b * (chunks // 2) + lax.div(j, 2))
-
-        for i in range(1, SUBS):
-            serve(i)
+                if odd == 0 and not first:
+                    @pl.when(w == 2)
+                    def _():
+                        finish(0, 2)
+
+                    @pl.when(w > 2)
+                    def _():
+                        finish(w - 2, 1)
+
+                for i in mine:
+                    serve(w, i, count)
+
+    unit(jnp.int32(0), 2, True, False)
+
+    def steady(w, carry):
+        unit(w, 1, False, False)
         return carry
 
-    lax.fori_loop(0, ticks, tick, 0)
+    lax.fori_loop(1, units - 1, steady, 0)
+    unit(jnp.int32(units - 1), LAST, False, True)
+
+    def each_copy(visit):
+        for i in range(2):
+            visit(jnp.int32(0), i, 2)
+
+        def middle(w, carry):
+            visit(w, 0, 1)
+            return carry
+
+        lax.fori_loop(1, units - 1, middle, 0)
+        for i in range(LAST):
+            visit(jnp.int32(units - 1), i, LAST)
 
     @pl.when(is_inner)
     def _():
-        for u in range(copies - LAG, copies):
-            finish(u)
-
-        def drain(t, carry):
-            pair_copy(t).wait_send()
-            final_copy(t).wait_send()
-            return carry
-
-        lax.fori_loop(0, copies, drain, 0)
+        finish(jnp.int32(units - 2), 1)
+        finish(jnp.int32(units - 1), LAST)
+
+        def drain(*where):
+            pair_copy(*where).wait_send()
+            final_copy(*where).wait_send()
+
+        each_copy(drain)
 
     @pl.when(is_outer)
     def _():
-        def drain(t, carry):
-            partial_copy(t).wait_send()
-            final_copy(t).wait_recv()
-            return carry
-
-        lax.fori_loop(0, copies, drain, 0)
+        def drain(*where):
+            partial_copy(*where).wait_send()
+            final_copy(*where).wait_recv()
+
+        each_copy(drain)
 
     for part_id in range(4):
         @pl.when(cp == 0)
@@ -430,17 +457,18 @@
         q_tiles = depth // TILE
         kv_cols = w_key.shape[1]
         br = rows // BLOCKS
-        copies = SUBS * BLOCKS * (width // COLS)
+        copies = BLOCKS * (width // COLS) // 2 + 5
         any_spec = pl.BlockSpec(memory_space=pl.ANY)
         vmem_spec = pl.BlockSpec(memory_space=pltpu.VMEM)
         bf16, f32 = jnp.bfloat16, jnp.float32
         dma = pltpu.SemaphoreType.DMA
-        held = 2 * rows * (width + 2 * TILE)
+        held = 2 * rows * (width + 2 * TILE) + 8 * rows * HEAD
+        cos_t, sin_t = (pltpu.with_memory_space_constraint(t, pltpu.VMEM) for t in rope_tables(positions))
         out, keys, values = pl.pallas_call(
             block_kernel,
             out_shape=(pltpu.VMEM((rows, width), bf16), pltpu.VMEM((2, rows, HEAD), bf16),
                        pltpu.VMEM((2, rows, HEAD), bf16)),
-            in_specs=[any_spec] * 8,
+            in_specs=[any_spec, any_spec, vmem_spec, vmem_spec] + [any_spec] * 4,
             out_specs=(vmem_spec, vmem_spec, vmem_spec),
             scratch_shapes=[
                 pltpu.VMEM((rows, width), bf16),
@@ -451,22 +479,20 @@
                 pltpu.VMEM((4, 4, rows, HEAD), bf16),
                 pltpu.VMEM((2, q_tiles, br, TILE), bf16),
                 pltpu.VMEM((rows // 2, TILE), f32),
-                pltpu.VMEM((br, COLS), f32),
+                pltpu.VMEM((br, 2 * COLS), f32),
                 pltpu.VMEM((rows, width), bf16),
                 pltpu.VMEM((rows, HEAD), f32),
                 pltpu.VMEM((rows, HEAD), f32),
                 pltpu.VMEM((width // HEAD, HEAD), bf16),
                 pltpu.VMEM((1, width), f32),
-                pltpu.VMEM((rows, HEAD // 2), f32),
-                pltpu.VMEM((rows, HEAD // 2), f32),
                 pltpu.VMEM((rows, HEAD), f32),
-                dma((3,)), dma((PIECES,)), dma((RING, 4)), dma((4,)), dma((4, 2)), dma((4, 4)),
+                dma, dma((PIECES,)), dma((RING, 4)), dma((4,)), dma((4, 2)), dma((4, 4)),
                 dma((copies,)), dma((copies,)), dma((copies,)), dma((copies,)),
             ],
             compiler_params=pltpu.CompilerParams(collective_id=0, has_side_effects=True,
                                                  vmem_limit_bytes=67043328 - held - 65536),
             name="attention_block",
-        )(hidden, norm_gain.reshape(width // HEAD, HEAD), *rope_tables(positions), w_query, w_key, w_value, w_out)
+        )(hidden, norm_gain.reshape(width // HEAD, HEAD), cos_t, sin_t, w_query, w_key, w_value, w_out)
         return out, jnp.transpose(keys, (1, 0, 2)), jnp.transpose(values, (1, 0, 2))
 
     return jax.shard_map(local_block, mesh=mesh, in_specs=(row_spec, P(('dp', 'cp')), P(None), head_cols, head_cols, head_cols, P('tp', None)), out_specs=(row_spec, cache_spec, cache_spec), check_vma=False)

time: 241 us -> 243 us (level)
  no operation moved by 1% of the time
where the time goes in v5:
time: 243 us
  Pallas kernels  235 us (97%)
  local copies, waits for them, and re-layouts  5.34 us (2%)
    pallas_call x1, Pallas kernels, local_block(): pl.pallas_call(block_kernel, out_shape=(pltpu.VMEM((rows, width), bf16),...  235 us
    unnamed x3, local copies, waits for them, and re-layouts  5.34 us

profile of v5, /device:TPU:7, one launch (start us, length us, event | category | flops | bytes accessed | tf_op | source)
XLA Modules:
  0.0 242.7 jit_solution(2431557591902358498)
XLA Ops:
  0.6 0.7 convert_element_type.3
  1.3 1.0 multiply_sine_fusion
  2.3 235.0 %attention_block.1 = (bf16[512,8192]{1,0:T(8,128)(2,1)S(1)}, bf16[2,512,128]{2,1,0:T(8,128)(2,1)S(1)}, bf16[2,512,128]{2,1,0:T(8,128)(2,1)S(1)}) custom-call(bf16[512,8192]{1,0:T(8,128)(2,1)} %hidden.1, bf16[64,128]{1,0:T(8,128)(2,1)} %bitcast.5, f32[512,64]{1,0:T(8,128)S(1)} %get-tuple-element.13.cos_in, f32[512,64]{1,0:T(8,128)S(1)} %get-tuple-element.12.sin_in, ...), custom_call_target="tpu_custom_call" | custom-call | tf_op jit(solution)/shard_map/attention_block/pallas_call | solution.py:467
  237.3 3.4 %copy.13 = bf16[512,8192]{1,0:T(8,128)(2,1)} copy(bf16[512,8192]{1,0:T(8,128)(2,1)S(1)} %get-tuple-element.14) | data formatting | bytes 16777216
  240.7 1.0 copy.10
  241.7 1.0 copy.11
  (1 shorter events, 0.0 us)

commit v6 on v4

--- a/solution.py
+++ b/solution.py
@@ -31,10 +31,10 @@
 def block_kernel(hidden, gain, cos_in, sin_in, w_query, w_key, w_value, w_out,
                  buf_b, k_out, v_out,
                  xbuf, hbuf, wbuf, w_late, qbuf, kvbuf, obuf, acc, part, buf_a, cos_ref, sin_ref,
-                 gain_raw, gain_row, cos_half, sin_half, inv_ref, small_sem, xsem, wsem, late_sem, kv_send, kv_recv, send_a, recv_a, send_b, recv_b):
+                 gain_raw, gain_row, inv_ref, small_sem, xsem, wsem, late_sem, kv_send, kv_recv, send_a, recv_a, send_b, recv_b):
     rows, width = xbuf.shape
     q_tiles = qbuf.shape[0]
-    depth = wbuf.shape[1] // 4
+    depth = wbuf.shape[1]
     br = rows // BLOCKS
     piece_rows = rows // PIECES
     half = rows // 2
@@ -50,40 +50,28 @@
         sl = pl.ds(b * piece_rows, piece_rows)
         return pltpu.make_async_copy(hidden.at[sl, :], xbuf.at[sl, :], xsem.at[b])
 
-    def col_tile(w_ref, col, slot, piece):
-        return pltpu.make_async_copy(w_ref.at[pl.ds(piece * depth, depth), pl.ds(col, TILE)],
-                                     wbuf.at[slot, pl.ds(piece * depth, depth)], wsem.at[slot, piece])
-
-    def late_tile(j, piece):
-        return pltpu.make_async_copy(
-            w_query.at[pl.ds(piece * depth, depth), pl.ds(pl.multiple_of(j * TILE, TILE), TILE)],
-            w_late.at[pl.ds(piece * depth, depth)], late_sem.at[piece])
-
-    def out_tile(col, slot, piece):
-        return pltpu.make_async_copy(w_out.at[:, pl.ds(col + piece * TILE, TILE)],
-                                     wbuf.at[slot, pl.ds(piece * depth, depth)], wsem.at[slot, piece])
-
-    def start_key():
-        for piece in range(4):
-            col_tile(w_key, 0, 0, piece).start()
-
-    def start_value():
-        for piece in range(4):
-            col_tile(w_value, 0, 1, piece).start()
-
-    def start_query(j):
-        for piece in range(4):
-            col_tile(w_query, pl.multiple_of(j * TILE, TILE), lax.rem(j + 2, RING), piece).start()
-
-    def start_out(t):
+    def kv_tile(w_ref, slot, piece):
+        return pltpu.make_async_copy(w_ref.at[pl.ds(piece * depth, depth), :],
+                                     wbuf.at[slot, :, pl.ds(piece * TILE, TILE)], wsem.at[slot, piece])
+
+    def query_block(i):
+        return w_query.at[pl.ds(pl.multiple_of(lax.rem(i, 4) * depth, depth), depth),
+                          pl.ds(pl.multiple_of(lax.div(i, 4) * COLS, COLS), COLS)]
+
+    def query_tile(i):
+        slot = lax.rem(i + 2, RING)
+        return pltpu.make_async_copy(query_block(i), wbuf.at[slot], wsem.at[slot, 0])
+
+    def late_tile(i):
+        return pltpu.make_async_copy(query_block(i), w_late, late_sem)
+
+    def out_tile(t):
+        slot = lax.rem(t + 2 + q_tiles, RING)
         col = pl.multiple_of(lax.rem(t, chunks) * COLS, COLS)
-        for piece in range(4):
-            out_tile(col, lax.rem(t + 2 + q_tiles, RING), piece).start()
-
-    small = (pltpu.make_async_copy(gain, gain_raw, small_sem.at[0]),
-             pltpu.make_async_copy(cos_in, cos_half, small_sem.at[1]),
-             pltpu.make_async_copy(sin_in, sin_half, small_sem.at[2]))
-    small[0].start()
+        return pltpu.make_async_copy(w_out.at[:, pl.ds(col, COLS)], wbuf.at[slot], wsem.at[slot, 0])
+
+    gain_copy = pltpu.make_async_copy(gain, gain_raw, small_sem)
+    gain_copy.start()
     for b in range(3):
         x_copy(b).start()
 
@@ -91,7 +79,7 @@
     for peer in ({"cp": cp ^ 1}, {"cp": cp ^ 2}, {"tp": tp ^ 1}, {"tp": 3 - tp}):
         pl.semaphore_signal(barrier, inc=1, device_id=peer, device_id_type=MESH)
 
-    small[0].wait()
+    gain_copy.wait()
     for c in range(width // HEAD):
         gain_row[:, c * HEAD:(c + 1) * HEAD] = gain_raw[c:c + 1, :].astype(jnp.float32)
 
@@ -118,8 +106,29 @@
 
         lax.fori_loop(0, piece_rows // 16, norm_rows, 0)
 
-    def project(w_ref, first):
-        acc[...] = jnp.dot(hbuf[pl.ds(first, half), :], w_ref[...], preferred_element_type=jnp.float32)
+    def project_kv(slot, first):
+        prods = [jnp.dot(hbuf[pl.ds(first, half), piece * depth:(piece + 1) * depth],
+                         wbuf[slot, :, piece * TILE:(piece + 1) * TILE], preferred_element_type=jnp.float32)
+                 for piece in range(4)]
+        acc[:, :TILE] = (prods[0] + prods[1]) + (prods[2] + prods[3])
+
+    def project_query(w_ref, first, i):
+        quarter = lax.rem(i, 4)
+        prod = jnp.dot(hbuf[pl.ds(first, half), pl.ds(pl.multiple_of(quarter * depth, depth), depth)],
+                       w_ref[...], preferred_element_type=jnp.float32)
+
+        @pl.when(quarter == 0)
+        def _():
+            acc[...] = prod
+
+        @pl.when(quarter > 0)
+        def _():
+            acc[...] += prod
+
+        @pl.when(quarter == 3)
+        def _():
+            for head in range(COLS // HEAD):
+                qbuf[lax.div(i, 4) * (COLS // TILE) + head // 2, head % 2, first:first + half] = roped(head, first)
 
     def roped(head, first):
         vals = acc[:, head * HEAD:(head + 1) * HEAD]
@@ -164,24 +173,22 @@
             if b + 3 < PIECES:
                 x_copy(b + 3).start()
             if b == 0:
-                start_key()
+                for piece in range(4):
+                    kv_tile(w_key, 0, piece).start()
             elif b == 1:
-                start_value()
-                small[1].start()
-                small[2].start()
+                for piece in range(4):
+                    kv_tile(w_value, 1, piece).start()
             elif b in (PIECES // 2, PIECES // 2 + 1):
-                start_query(b - PIECES // 2)
+                query_tile(jnp.int32(b - PIECES // 2)).start()
             normalize(b)
         if hf == 0:
-            small[1].wait()
-            small[2].wait()
-            cos_ref[...] = jnp.concatenate([cos_half[...], cos_half[...]], axis=1)
-            sin_ref[...] = jnp.concatenate([-sin_half[...], sin_half[...]], axis=1)
+            cos_ref[...] = jnp.concatenate([cos_in[...], cos_in[...]], axis=1)
+            sin_ref[...] = jnp.concatenate([-sin_in[...], sin_in[...]], axis=1)
             for piece in range(4):
-                col_tile(w_key, 0, 0, piece).wait()
-        project(wbuf.at[0], first)
+                kv_tile(w_key, 0, piece).wait()
+        project_kv(0, first)
         if hf == 1:
-            start_query(2)
+            query_tile(jnp.int32(2)).start()
         for head in range(2):
             key = roped(head, first)
             kvbuf[cp, head, first:first + half] = key
@@ -189,36 +196,30 @@
         if hf == 0:
             pl.semaphore_wait(barrier, 4)
             for piece in range(4):
-                col_tile(w_value, 0, 1, piece).wait()
+                kv_tile(w_value, 1, piece).wait()
         send_own(2 * hf)
-        project(wbuf.at[1], first)
+        project_kv(1, first)
         if hf == 1:
-            start_query(3)
+            query_tile(jnp.int32(3)).start()
         for head in range(2):
             value = acc[:, head * HEAD:(head + 1) * HEAD].astype(jnp.bfloat16)
             kvbuf[cp, 2 + head, first:first + half] = value
             v_out[head, first:first + half] = value
         send_own(2 * hf + 1)
 
-    for piece in range(4):
-        late_tile(0, piece).start()
+    late_tile(jnp.int32(0)).start()
 
     def query_step(j, carry):
-        slot = lax.rem(j + 2, RING)
-        for piece in range(4):
-            col_tile(w_query, pl.multiple_of(j * TILE, TILE), slot, piece).wait()
-        project(wbuf.at[slot], 0)
+        query_tile(j).wait()
+        project_query(wbuf.at[lax.rem(j + 2, RING)], 0, j)
 
         @pl.when(j + RING < q_tiles)
         def _():
-            start_query(j + RING)
+            query_tile(j + RING).start()
 
         @pl.when(j + RING >= q_tiles)
         def _():
-            start_out(j + RING - q_tiles)
-
-        for head in range(2):
-            qbuf[j, head, :half] = roped(head, 0)
+            out_tile(j + RING - q_tiles).start()
 
         for part_id in range(4):
             @pl.when(j == part_id * q_tiles // 4)
@@ -244,17 +245,12 @@
             kv_copy(0, part_id, 0, 0).wait_recv()
 
     def late_queries(j):
-        for piece in range(4):
-            late_tile(j, piece).wait()
-        project(w_late, half)
+        late_tile(j).wait()
+        project_query(w_late, half, j)
 
         @pl.when(j + 1 < q_tiles)
         def _():
-            for piece in range(4):
-                late_tile(j + 1, piece).start()
-
-        for head in range(2):
-            qbuf[j, head, half:] = roped(head, half)
+            late_tile(j + 1).start()
 
     def attend(b, j):
         kv_head = lax.div(4 * j, group)
@@ -328,18 +324,13 @@
 
     def tick(t, carry):
         b, j = lax.div(t, chunks), lax.rem(t, chunks)
-        slot = lax.rem(t + 2 + q_tiles, RING)
-        col = pl.multiple_of(j * COLS, COLS)
-        for piece in range(4):
-            out_tile(col, slot, piece).wait()
+        out_tile(t).wait()
         lhs = jnp.concatenate([obuf[lax.rem(b, 2), i] for i in range(q_tiles)], axis=1)
-        for piece in range(4):
-            part[:, piece * TILE:(piece + 1) * TILE] = jnp.dot(lhs, wbuf[slot, piece * depth:(piece + 1) * depth],
-                                                              preferred_element_type=jnp.float32)
+        part[...] = jnp.dot(lhs, wbuf[lax.rem(t + 2 + q_tiles, RING)], preferred_element_type=jnp.float32)
 
         @pl.when(t + RING < ticks)
         def _():
-            start_out(t + RING)
+            out_tile(t + RING).start()
 
         @pl.when(is_outer)
         def _():
@@ -435,38 +426,37 @@
         vmem_spec = pl.BlockSpec(memory_space=pltpu.VMEM)
         bf16, f32 = jnp.bfloat16, jnp.float32
         dma = pltpu.SemaphoreType.DMA
-        held = 2 * rows * (width + 2 * TILE)
+        held = 2 * rows * (width + 2 * TILE) + 8 * rows * HEAD
+        cos_t, sin_t = (pltpu.with_memory_space_constraint(t, pltpu.VMEM) for t in rope_tables(positions))
         out, keys, values = pl.pallas_call(
             block_kernel,
             out_shape=(pltpu.VMEM((rows, width), bf16), pltpu.VMEM((2, rows, HEAD), bf16),
                        pltpu.VMEM((2, rows, HEAD), bf16)),
-            in_specs=[any_spec] * 8,
+            in_specs=[any_spec, any_spec, vmem_spec, vmem_spec] + [any_spec] * 4,
             out_specs=(vmem_spec, vmem_spec, vmem_spec),
             scratch_shapes=[
                 pltpu.VMEM((rows, width), bf16),
                 pltpu.VMEM((rows, width), bf16),
-                pltpu.VMEM((RING, width, TILE), bf16),
-                pltpu.VMEM((width, TILE), bf16),
+                pltpu.VMEM((RING, depth, COLS), bf16),
+                pltpu.VMEM((depth, COLS), bf16),
                 pltpu.VMEM((q_tiles, 2, rows, HEAD), bf16),
                 pltpu.VMEM((4, 4, rows, HEAD), bf16),
                 pltpu.VMEM((2, q_tiles, br, TILE), bf16),
-                pltpu.VMEM((rows // 2, TILE), f32),
+                pltpu.VMEM((rows // 2, COLS), f32),
                 pltpu.VMEM((br, COLS), f32),
                 pltpu.VMEM((rows, width), bf16),
                 pltpu.VMEM((rows, HEAD), f32),
                 pltpu.VMEM((rows, HEAD), f32),
                 pltpu.VMEM((width // HEAD, HEAD), bf16),
                 pltpu.VMEM((1, width), f32),
-                pltpu.VMEM((rows, HEAD // 2), f32),
-                pltpu.VMEM((rows, HEAD // 2), f32),
                 pltpu.VMEM((rows, HEAD), f32),
-                dma((3,)), dma((PIECES,)), dma((RING, 4)), dma((4,)), dma((4, 2)), dma((4, 4)),
+                dma, dma((PIECES,)), dma((RING, 4)), dma, dma((4, 2)), dma((4, 4)),
                 dma((copies,)), dma((copies,)), dma((copies,)), dma((copies,)),
             ],
             compiler_params=pltpu.CompilerParams(collective_id=0, has_side_effects=True,
                                                  vmem_limit_bytes=67043328 - held - 65536),
             name="attention_block",
-        )(hidden, norm_gain.reshape(width // HEAD, HEAD), *rope_tables(positions), w_query, w_key, w_value, w_out)
+        )(hidden, norm_gain.reshape(width // HEAD, HEAD), cos_t, sin_t, w_query, w_key, w_value, w_out)
         return out, jnp.transpose(keys, (1, 0, 2)), jnp.transpose(values, (1, 0, 2))
 
     return jax.shard_map(local_block, mesh=mesh, in_specs=(row_spec, P(('dp', 'cp')), P(None), head_cols, head_cols, head_cols, P('tp', None)), out_specs=(row_spec, cache_spec, cache_spec), check_vma=False)

time: 241 us -> 240 us (level)
  no operation moved by 1% of the time
where the time goes in v6:
time: 240 us
  Pallas kernels  232 us (97%)
  local copies, waits for them, and re-layouts  5.34 us (2%)
    pallas_call x1, Pallas kernels, local_block(): pl.pallas_call(block_kernel, out_shape=(pltpu.VMEM((rows, width), bf16),...  232 us
    unnamed x3, local copies, waits for them, and re-layouts  5.34 us

profile of v6, /device:TPU:7, one launch (start us, length us, event | category | flops | bytes accessed | tf_op | source)
XLA Modules:
  0.0 240.0 jit_solution(16180912817167285899)
XLA Ops:
  0.6 0.7 convert_element_type.3
  1.3 1.0 multiply_sine_fusion
  2.3 232.4 %attention_block.1 = (bf16[512,8192]{1,0:T(8,128)(2,1)S(1)}, bf16[2,512,128]{2,1,0:T(8,128)(2,1)S(1)}, bf16[2,512,128]{2,1,0:T(8,128)(2,1)S(1)}) custom-call(bf16[512,8192]{1,0:T(8,128)(2,1)} %hidden.1, bf16[64,128]{1,0:T(8,128)(2,1)} %bitcast.5, f32[512,64]{1,0:T(8,128)S(1)} %get-tuple-element.13.cos_in, f32[512,64]{1,0:T(8,128)S(1)} %get-tuple-element.12.sin_in, ...), custom_call_target="tpu_custom_call" | custom-call | tf_op jit(solution)/shard_map/attention_block/pallas_call | solution.py:431
  234.7 3.4 %copy.13 = bf16[512,8192]{1,0:T(8,128)(2,1)} copy(bf16[512,8192]{1,0:T(8,128)(2,1)S(1)} %get-tuple-element.14) | data formatting | bytes 16777216
  238.1 1.0 copy.10
  239.1 1.0 copy.11
  (1 shorter events, 0.0 us)

commit v7 on v4

--- a/solution.py
+++ b/solution.py
@@ -31,7 +31,7 @@
 def block_kernel(hidden, gain, cos_in, sin_in, w_query, w_key, w_value, w_out,
                  buf_b, k_out, v_out,
                  xbuf, hbuf, wbuf, w_late, qbuf, kvbuf, obuf, acc, part, buf_a, cos_ref, sin_ref,
-                 gain_raw, gain_row, cos_half, sin_half, inv_ref, small_sem, xsem, wsem, late_sem, kv_send, kv_recv, send_a, recv_a, send_b, recv_b):
+                 gain_raw, gain_row, inv_ref, small_sem, xsem, wsem, late_sem, kv_send, kv_recv, send_a, recv_a, send_b, recv_b):
     rows, width = xbuf.shape
     q_tiles = qbuf.shape[0]
     depth = wbuf.shape[1] // 4
@@ -80,10 +80,8 @@
         for piece in range(4):
             out_tile(col, lax.rem(t + 2 + q_tiles, RING), piece).start()
 
-    small = (pltpu.make_async_copy(gain, gain_raw, small_sem.at[0]),
-             pltpu.make_async_copy(cos_in, cos_half, small_sem.at[1]),
-             pltpu.make_async_copy(sin_in, sin_half, small_sem.at[2]))
-    small[0].start()
+    gain_copy = pltpu.make_async_copy(gain, gain_raw, small_sem)
+    gain_copy.start()
     for b in range(3):
         x_copy(b).start()
 
@@ -91,7 +89,7 @@
     for peer in ({"cp": cp ^ 1}, {"cp": cp ^ 2}, {"tp": tp ^ 1}, {"tp": 3 - tp}):
         pl.semaphore_signal(barrier, inc=1, device_id=peer, device_id_type=MESH)
 
-    small[0].wait()
+    gain_copy.wait()
     for c in range(width // HEAD):
         gain_row[:, c * HEAD:(c + 1) * HEAD] = gain_raw[c:c + 1, :].astype(jnp.float32)
 
@@ -167,16 +165,12 @@
                 start_key()
             elif b == 1:
                 start_value()
-                small[1].start()
-                small[2].start()
             elif b in (PIECES // 2, PIECES // 2 + 1):
                 start_query(b - PIECES // 2)
             normalize(b)
         if hf == 0:
-            small[1].wait()
-            small[2].wait()
-            cos_ref[...] = jnp.concatenate([cos_half[...], cos_half[...]], axis=1)
-            sin_ref[...] = jnp.concatenate([-sin_half[...], sin_half[...]], axis=1)
+            cos_ref[...] = jnp.concatenate([cos_in[...], cos_in[...]], axis=1)
+            sin_ref[...] = jnp.concatenate([-sin_in[...], sin_in[...]], axis=1)
             for piece in range(4):
                 col_tile(w_key, 0, 0, piece).wait()
         project(wbuf.at[0], first)
@@ -185,7 +179,6 @@
         for head in range(2):
             key = roped(head, first)
             kvbuf[cp, head, first:first + half] = key
-            k_out[head, first:first + half] = key
         if hf == 0:
             pl.semaphore_wait(barrier, 4)
             for piece in range(4):
@@ -197,7 +190,6 @@
         for head in range(2):
             value = acc[:, head * HEAD:(head + 1) * HEAD].astype(jnp.bfloat16)
             kvbuf[cp, 2 + head, first:first + half] = value
-            v_out[head, first:first + half] = value
         send_own(2 * hf + 1)
 
     for piece in range(4):
@@ -383,6 +375,13 @@
         for u in range(copies - LAG, copies):
             finish(u)
 
+    for head in range(2):
+        k_out[:, head, :] = kvbuf[cp, head]
+        v_out[:, head, :] = kvbuf[cp, 2 + head]
+
+    @pl.when(is_inner)
+    def _():
+
         def drain(t, carry):
             pair_copy(t).wait_send()
             final_copy(t).wait_send()
@@ -417,6 +416,18 @@
         @pl.when(cp == 3)
         def _():
             kv_copy(1, part_id, 1, 2).wait_send()
+
+
+def store_kernel(out, keys, values, out_hbm, k_hbm, v_hbm, sems):
+    piece = out.shape[0] // PIECES
+    moves = [pltpu.make_async_copy(out.at[pl.ds(i * piece, piece)], out_hbm.at[pl.ds(i * piece, piece)], sems.at[i])
+             for i in range(PIECES)]
+    moves.append(pltpu.make_async_copy(keys, k_hbm, sems.at[PIECES]))
+    moves.append(pltpu.make_async_copy(values, v_hbm, sems.at[PIECES + 1]))
+    for move in moves:
+        move.start()
+    for move in moves:
+        move.wait()
 
 
 def solution(mesh):
@@ -435,12 +446,13 @@
         vmem_spec = pl.BlockSpec(memory_space=pltpu.VMEM)
         bf16, f32 = jnp.bfloat16, jnp.float32
         dma = pltpu.SemaphoreType.DMA
-        held = 2 * rows * (width + 2 * TILE)
+        held = 2 * rows * (width + 2 * TILE) + 8 * rows * HEAD
+        cos_t, sin_t = (pltpu.with_memory_space_constraint(t, pltpu.VMEM) for t in rope_tables(positions))
         out, keys, values = pl.pallas_call(
             block_kernel,
-            out_shape=(pltpu.VMEM((rows, width), bf16), pltpu.VMEM((2, rows, HEAD), bf16),
-                       pltpu.VMEM((2, rows, HEAD), bf16)),
-            in_specs=[any_spec] * 8,
+            out_shape=(pltpu.VMEM((rows, width), bf16), pltpu.VMEM((rows, 2, HEAD), bf16),
+                       pltpu.VMEM((rows, 2, HEAD), bf16)),
+            in_specs=[any_spec, any_spec, vmem_spec, vmem_spec] + [any_spec] * 4,
             out_specs=(vmem_spec, vmem_spec, vmem_spec),
             scratch_shapes=[
                 pltpu.VMEM((rows, width), bf16),
@@ -457,16 +469,23 @@
                 pltpu.VMEM((rows, HEAD), f32),
                 pltpu.VMEM((width // HEAD, HEAD), bf16),
                 pltpu.VMEM((1, width), f32),
-                pltpu.VMEM((rows, HEAD // 2), f32),
-                pltpu.VMEM((rows, HEAD // 2), f32),
                 pltpu.VMEM((rows, HEAD), f32),
-                dma((3,)), dma((PIECES,)), dma((RING, 4)), dma((4,)), dma((4, 2)), dma((4, 4)),
+                dma, dma((PIECES,)), dma((RING, 4)), dma((4,)), dma((4, 2)), dma((4, 4)),
                 dma((copies,)), dma((copies,)), dma((copies,)), dma((copies,)),
             ],
             compiler_params=pltpu.CompilerParams(collective_id=0, has_side_effects=True,
                                                  vmem_limit_bytes=67043328 - held - 65536),
             name="attention_block",
-        )(hidden, norm_gain.reshape(width // HEAD, HEAD), *rope_tables(positions), w_query, w_key, w_value, w_out)
-        return out, jnp.transpose(keys, (1, 0, 2)), jnp.transpose(values, (1, 0, 2))
+        )(hidden, norm_gain.reshape(width // HEAD, HEAD), cos_t, sin_t, w_query, w_key, w_value, w_out)
+        held_results = [pltpu.with_memory_space_constraint(t, pltpu.VMEM) for t in (out, keys, values)]
+        return pl.pallas_call(
+            store_kernel,
+            out_shape=tuple(jax.ShapeDtypeStruct(t.shape, bf16) for t in held_results),
+            in_specs=[vmem_spec] * 3,
+            out_specs=(any_spec,) * 3,
+            scratch_shapes=[dma((PIECES + 2,))],
+            compiler_params=pltpu.CompilerParams(vmem_limit_bytes=1 << 20),
+            name="store_results",
+        )(*held_results)
 
     return jax.shard_map(local_block, mesh=mesh, in_specs=(row_spec, P(('dp', 'cp')), P(None), head_cols, head_cols, head_cols, P('tp', None)), out_specs=(row_spec, cache_spec, cache_spec), check_vma=False)

time: 241 us -> 238 us (0.988)
  local copies, waits for them, and re-layouts: 5.34 us -> 0 us
    unnamed x3 -> x0, local copies, waits for them, and re-layouts: 5.34 us -> none
    pallas_call x0 -> x1, Pallas kernels: none -> 3.51 us  [local_block(): pl.pallas_call(store_kernel, out_shape=tuple((jax.ShapeDtypeStruct(t.shap...]
where the time goes in v7:
time: 238 us
  Pallas kernels  235 us (99%)
    pallas_call x1, Pallas kernels, local_block(): pl.pallas_call(block_kernel, out_shape=(pltpu.VMEM((rows, width), bf16),...  232 us

profile of v7, /device:TPU:7, one launch (start us, length us, event | category | flops | bytes accessed | tf_op | source)
XLA Modules:
  0.0 237.5 jit_solution(2679378019969997629)
XLA Ops:
  0.6 0.7 convert_element_type.3
  1.3 1.0 multiply_sine_fusion
  2.3 231.5 %attention_block.1 = (bf16[512,8192]{1,0:T(8,128)(2,1)S(1)}, bf16[512,2,128]{2,1,0:T(2,128)(2,1)S(1)}, bf16[512,2,128]{2,1,0:T(2,128)(2,1)S(1)}) custom-call(bf16[512,8192]{1,0:T(8,128)(2,1)} %hidden.1, bf16[64,128]{1,0:T(8,128)(2,1)} %bitcast.1, f32[512,64]{1,0:T(8,128)S(1)} %get-tuple-element.10.cos_in, f32[512,64]{1,0:T(8,128)S(1)} %get-tuple-element.9.sin_in, ...), custom_call_target="tpu_custom_call" | custom-call | tf_op jit(solution)/shard_map/attention_block/pallas_call | solution.py:451
  233.8 3.5 %store_results.1 = (bf16[512,8192]{1,0:T(8,128)(2,1)}, bf16[512,2,128]{2,1,0:T(2,128)(2,1)}, bf16[512,2,128]{2,1,0:T(2,128)(2,1)}) custom-call(bf16[512,8192]{1,0:T(8,128)(2,1)S(1)} %get-tuple-element.6.out, bf16[512,2,128]{2,1,0:T(2,128)(2,1)S(1)} %get-tuple-element.7.keys, bf16[512,2,128]{2,1,0:T(2,128)(2,1)S(1)} %get-tuple-element.8.values), custom_call_target="tpu_custom_call" | custom-call | tf_op jit(solution)/shard_map/store_results/pallas_call | solution.py:481
  (1 shorter events, 0.0 us)

commit v8 on v7

--- a/solution.py
+++ b/solution.py
@@ -212,7 +212,7 @@
         for head in range(2):
             qbuf[j, head, :half] = roped(head, 0)
 
-        for part_id in range(4):
+        for part_id in range(3):
             @pl.when(j == part_id * q_tiles // 4)
             def _():
                 relay(part_id)
@@ -220,20 +220,22 @@
         return carry
 
     lax.fori_loop(0, q_tiles, query_step, 0)
-
-    for part_id in range(4):
-        @pl.when(cp == 1)
-        def _():
-            kv_copy(0, part_id, 0, 0).wait_recv()
-
-        @pl.when(cp == 2)
-        def _():
-            kv_copy(1, part_id, 0, 0).wait_recv()
-
-        @pl.when(cp == 3)
-        def _():
+    relay(3)
+
+    @pl.when(cp == 3)
+    def _():
+        for part_id in range(4):
             kv_copy(2, part_id, 0, 0).wait_recv()
-            kv_copy(0, part_id, 0, 0).wait_recv()
+
+    def await_last_slot():
+        for part_id in range(4):
+            @pl.when(jnp.logical_or(cp == 1, cp == 3))
+            def _():
+                kv_copy(0, part_id, 0, 0).wait_recv()
+
+            @pl.when(cp == 2)
+            def _():
+                kv_copy(1, part_id, 0, 0).wait_recv()
 
     def late_queries(j):
         for piece in range(4):
@@ -248,45 +250,54 @@
         for head in range(2):
             qbuf[j, head, half:] = roped(head, half)
 
-    def attend(b, j):
-        kv_head = lax.div(4 * j, group)
-        qs = qbuf[pl.ds(2 * j, 2), :, pl.ds(pl.multiple_of(b * br, br), br), :].reshape(4 * br, HEAD)
-
-        def scores_of(slot):
-            return lax.dot_general(qs, kvbuf[slot, kv_head], (((1,), (1,)), ((), ())),
+    def attend(b, js, gate=None):
+        kv_heads = [lax.div(4 * j, group) for j in js]
+        qs = [qbuf[pl.ds(2 * j, 2), :, pl.ds(pl.multiple_of(b * br, br), br), :].reshape(4 * br, HEAD) for j in js]
+
+        def scores_of(n, slot):
+            return lax.dot_general(qs[n], kvbuf[slot, kv_heads[n]], (((1,), (1,)), ((), ())),
                                    preferred_element_type=jnp.float32)
 
-        scores = scores_of(cp)
-        row = lax.broadcasted_iota(jnp.int32, scores.shape, 0) % br + b * br
-        key = lax.broadcasted_iota(jnp.int32, scores.shape, 1)
-        scores = jnp.where(key <= row, scores, -jnp.inf)
-        top = jnp.max(scores, axis=-1, keepdims=True)
-        probs = jnp.exp2((scores - top) * EXP2_SCALE)
-        total = jnp.sum(probs, axis=-1, keepdims=True)
-        mixed = jnp.dot(probs.astype(jnp.bfloat16), kvbuf[cp, 2 + kv_head], preferred_element_type=jnp.float32)
-
-        def earlier(slot, carry):
-            top, total, mixed = carry
-            scores = scores_of(slot)
-            new_top = jnp.maximum(top, jnp.max(scores, axis=-1, keepdims=True))
-            fade = jnp.exp2((top - new_top) * EXP2_SCALE)
-            probs = jnp.exp2((scores - new_top) * EXP2_SCALE)
-            total = total * fade + jnp.sum(probs, axis=-1, keepdims=True)
-            mixed = mixed * fade + jnp.dot(probs.astype(jnp.bfloat16), kvbuf[slot, 2 + kv_head],
-                                           preferred_element_type=jnp.float32)
-            return new_top, total, mixed
-
-        top, total, mixed = lax.fori_loop(0, cp, earlier, (top, total, mixed))
-        attn = (mixed / total).astype(jnp.bfloat16)
-        for i in range(2):
-            obuf[lax.rem(b, 2), 2 * j + i] = jnp.concatenate(
-                [attn[2 * i * br:(2 * i + 1) * br], attn[(2 * i + 1) * br:(2 * i + 2) * br]], axis=1)
-
-    def first_block(j, carry):
-        attend(0, j)
+        def mix(n, slot, probs):
+            return jnp.dot(probs.astype(jnp.bfloat16), kvbuf[slot, 2 + kv_heads[n]],
+                           preferred_element_type=jnp.float32)
+
+        stats = []
+        for n in range(len(js)):
+            scores = scores_of(n, cp)
+            row = lax.broadcasted_iota(jnp.int32, scores.shape, 0) % br + b * br
+            key = lax.broadcasted_iota(jnp.int32, scores.shape, 1)
+            scores = jnp.where(key <= row, scores, -jnp.inf)
+            top = jnp.max(scores, axis=-1, keepdims=True)
+            probs = jnp.exp2((scores - top) * EXP2_SCALE)
+            stats.append((top, jnp.sum(probs, axis=-1, keepdims=True), mix(n, cp, probs)))
+
+        def earlier(i, carry):
+            slot = i + lax.div(cp, 3) * (2 - 2 * i)
+            if gate is not None:
+                pl.when(jnp.logical_and(gate, i == cp - 1))(await_last_slot)
+            out = []
+            for n, (top, total, mixed) in enumerate(carry):
+                scores = scores_of(n, slot)
+                new_top = jnp.maximum(top, jnp.max(scores, axis=-1, keepdims=True))
+                fade = jnp.exp2((top - new_top) * EXP2_SCALE)
+                probs = jnp.exp2((scores - new_top) * EXP2_SCALE)
+                out.append((new_top, total * fade + jnp.sum(probs, axis=-1, keepdims=True),
+                            mixed * fade + mix(n, slot, probs)))
+            return tuple(out)
+
+        stats = lax.fori_loop(0, cp, earlier, tuple(stats))
+        for j, (top, total, mixed) in zip(js, stats):
+            attn = (mixed / total).astype(jnp.bfloat16)
+            for i in range(2):
+                obuf[lax.rem(b, 2), 2 * j + i] = jnp.concatenate(
+                    [attn[2 * i * br:(2 * i + 1) * br], attn[(2 * i + 1) * br:(2 * i + 2) * br]], axis=1)
+
+    def first_block(p, carry):
+        attend(0, (2 * p, 2 * p + 1), gate=p == 0)
         return carry
 
-    lax.fori_loop(0, q_tiles // 2, first_block, 0)
+    lax.fori_loop(0, q_tiles // 4, first_block, 0)
 
     sub_cols = COLS // SUBS
     copies = ticks * SUBS
@@ -358,7 +369,7 @@
 
         @pl.when(jnp.logical_and(b + 1 < BLOCKS, lax.rem(j, 2) == 0))
         def _():
-            attend(b + 1, lax.div(j, 2))
+            attend(b + 1, (lax.div(j, 2),))
 
         @pl.when(jnp.logical_and(b < 2, lax.rem(j, 2) == 1))
         def _():

time: 238 us -> 237 us (level)
  no operation moved by 1% of the time
where the time goes in v8:
time: 237 us
  Pallas kernels  234 us (99%)
    pallas_call x1, Pallas kernels, local_block(): pl.pallas_call(block_kernel, out_shape=(pltpu.VMEM((rows, width), bf16),...  231 us

profile of v8, /device:TPU:7, one launch (start us, length us, event | category | flops | bytes accessed | tf_op | source)
XLA Modules:
  0.0 236.8 jit_solution(18056517869528933947)
XLA Ops:
  0.6 0.7 convert_element_type.3
  1.3 1.0 multiply_sine_fusion
  2.3 230.8 %attention_block.1 = (bf16[512,8192]{1,0:T(8,128)(2,1)S(1)}, bf16[512,2,128]{2,1,0:T(2,128)(2,1)S(1)}, bf16[512,2,128]{2,1,0:T(2,128)(2,1)S(1)}) custom-call(bf16[512,8192]{1,0:T(8,128)(2,1)} %hidden.1, bf16[64,128]{1,0:T(8,128)(2,1)} %bitcast.1, f32[512,64]{1,0:T(8,128)S(1)} %get-tuple-element.10.cos_in, f32[512,64]{1,0:T(8,128)S(1)} %get-tuple-element.9.sin_in, ...), custom_call_target="tpu_custom_call" | custom-call | tf_op jit(solution)/shard_map/attention_block/pallas_call | solution.py:462
  233.1 3.5 %store_results.1 = (bf16[512,8192]{1,0:T(8,128)(2,1)}, bf16[512,2,128]{2,1,0:T(2,128)(2,1)}, bf16[512,2,128]{2,1,0:T(2,128)(2,1)}) custom-call(bf16[512,8192]{1,0:T(8,128)(2,1)S(1)} %get-tuple-element.6.out, bf16[512,2,128]{2,1,0:T(2,128)(2,1)S(1)} %get-tuple-element.7.keys, bf16[512,2,128]{2,1,0:T(2,128)(2,1)S(1)} %get-tuple-element.8.values), custom_call_target="tpu_custom_call" | custom-call | tf_op jit(solution)/shard_map/store_results/pallas_call | solution.py:492
  (1 shorter events, 0.0 us)
